TPU v7x, 128 devices: a whole 4x4x4 slice. The times are simulated.
128 devices in a mesh: rep: 1, ep: 2 (over core), fsdp: 64 (over z, y, x).
Axes of the slice: x: 4, y: 4, z: 4, core: 2. Of those that a mesh axis runs over, the one named last changes fastest.
Arguments:
- x_in: bfloat16 [65536, 1024], P(('rep', 'ep', 'fsdp'))
- norm_w: float32 [2, 1024], replicated
- router_w: bfloat16 [2, 1024, 32], replicated
- gate_w: bfloat16 [2, 32, 1024, 512], P(None, 'ep', None, 'fsdp')
- up_w: bfloat16 [2, 32, 1024, 512], P(None, 'ep', None, 'fsdp')
- down_w: bfloat16 [2, 32, 512, 1024], P(None, 'ep', 'fsdp')
- routes: int32 [2, 65536, 8], P(None, ('rep', 'ep', 'fsdp'))
Outputs:
- output: bfloat16 [65536, 1024], P(('rep', 'ep', 'fsdp'))
All inputs are finite; a program needn't handle non-finite values.
Results may differ from a plain program's by a relative error of at most 0.00733116.
Values are sent between devices in bfloat16 or wider.
A program may use at most 1 GiB of HBM per device.

v0:
```python
import jax
import jax.numpy as jnp
from jax import lax
from jax.sharding import PartitionSpec as P

NORM_EPS = 1e-5


def rms_norm(stream, norm_row):
    widened = stream.astype(jnp.float32)
    inv_rms = lax.rsqrt(jnp.mean(widened * widened, axis=-1, keepdims=True) + NORM_EPS)
    return (widened * inv_rms * norm_row).astype(jnp.bfloat16)


def route_gates(hidden, router_l, routes_l):
    logits = jnp.dot(hidden, router_l, preferred_element_type=jnp.float32)
    return jax.nn.softmax(jnp.take_along_axis(logits, routes_l, axis=-1), axis=-1)


def capacity_of(tok_dev, top_k, experts):
    return 8 * ((2 * tok_dev * top_k + 8 * experts - 1) // (8 * experts))


def slot_plan(routes_l, experts, capacity, owners):
    tok_dev, top_k = routes_l.shape
    flat_ids = routes_l.reshape(-1)
    onehot = (flat_ids[:, None] == jnp.arange(experts, dtype=flat_ids.dtype)[None, :]).astype(jnp.int32)
    pair_rank = jnp.sum((jnp.cumsum(onehot, axis=0) - 1) * onehot, axis=1)
    n_local = experts // owners
    pair_slot = ((flat_ids % n_local) * owners + flat_ids // n_local) * capacity + pair_rank
    pair_token = jnp.arange(tok_dev * top_k, dtype=jnp.int32) // top_k
    slot_token = jnp.zeros((experts * capacity,), jnp.int32).at[pair_slot].set(pair_token)
    return pair_slot, slot_token


def expert_ffn(expert_rows, gate_full, up_full, down_full):
    pre_gate = jnp.einsum("erd,edf->erf", expert_rows, gate_full, preferred_element_type=jnp.float32)
    pre_up = jnp.einsum("erd,edf->erf", expert_rows, up_full, preferred_element_type=jnp.float32)
    inner_act = (jax.nn.silu(pre_gate) * pre_up).astype(jnp.bfloat16)
    return jnp.einsum("erf,efd->erd", inner_act, down_full, preferred_element_type=jnp.float32).astype(jnp.bfloat16)


def combine(stream, gate_probs, pair_out):
    mixed_sum = jnp.sum(gate_probs[..., None] * pair_out.astype(jnp.float32), axis=-2)
    return (stream.astype(jnp.float32) + mixed_sum).astype(jnp.bfloat16)


def solution(mesh):
    owners = mesh.shape["ep"]
    token_spec = P(("rep", "ep", "fsdp"), None)
    expert_in_spec = P(None, "ep", None, "fsdp")
    expert_out_spec = P(None, "ep", "fsdp", None)
    route_spec = P(None, ("rep", "ep", "fsdp"), None)

    def device_step(x_in, norm_w, router_w, gate_w, up_w, down_w, routes):
        layers, tok_dev, top_k = routes.shape
        experts = router_w.shape[2]
        n_local = gate_w.shape[1]
        d_model = x_in.shape[1]
        capacity = capacity_of(tok_dev, top_k, experts)
        stream = x_in
        for layer_idx in range(layers):
            routes_l = routes[layer_idx]
            hidden = rms_norm(stream, norm_w[layer_idx])
            gate_probs = route_gates(hidden, router_w[layer_idx], routes_l)
            pair_slot, slot_token = slot_plan(routes_l, experts, capacity, owners)
            send_buf = hidden[slot_token].reshape(n_local, owners, capacity, d_model)
            recv_buf = lax.all_to_all(send_buf, "ep", 1, 1, tiled=True)
            gate_full = lax.all_gather(gate_w[layer_idx], "fsdp", axis=2, tiled=True)
            up_full = lax.all_gather(up_w[layer_idx], "fsdp", axis=2, tiled=True)
            down_full = lax.all_gather(down_w[layer_idx], "fsdp", axis=1, tiled=True)
            expert_out = expert_ffn(recv_buf.reshape(n_local, owners * capacity, d_model), gate_full, up_full, down_full)
            back_buf = lax.all_to_all(expert_out.reshape(n_local, owners, capacity, d_model), "ep", 1, 1, tiled=True)
            pair_out = back_buf.reshape(experts * capacity, d_model)[pair_slot].reshape(tok_dev, top_k, d_model)
            stream = combine(stream, gate_probs, pair_out)
        return stream

    return jax.shard_map(device_step, mesh=mesh,
                         in_specs=(token_spec, P(), P(), expert_in_spec, expert_in_spec, expert_out_spec, route_spec),
                         out_specs=token_spec, check_vma=False)
```

profile of v0, /device:TPU:1, one launch (start us, length us, event | category | flops | bytes accessed | tf_op | source)
XLA Modules:
  0.0 771.2 jit_solution(3134108358878456740)
XLA Ops:
  16.3 9.2 %reduce-window.14 = s32[32,32,128]{2,1,0:T(8,128)S(1)} reduce-window(s32[32,32,128]{2,1,0:T(8,128)S(1)} %fusion.46, s32[]{:T(128)} %constant.87.clone.1), window={size=1x1x128 pad=0_0x0_0x127_0}, to_apply=%region_3.0 | reduce-window | flops 16646144 | bytes 1048580 | tf_op jit(solution)/shard_map/reduce-window
  27.2 15.5 %scatter_custom_fusion = s32[8192]{0:T(1024)S(1)} fusion(s32[4096]{0:T(1024)S(1)} %bitcast.142, s32[4096]{0:T(1024)S(1)} %add_select_fusion, s32[]{:T(128)} %constant.87.clone.1), kind=kCustom, calls=%fused_computation.107 | custom fusion | bytes 32772 | tf_op jit(solution)/shard_map/scatter | solution.py:32
  47.2 35.4 %gather_fusion = bf16[8192,1024]{1,0:T(8,128)(2,1)} fusion(bf16[512,1024]{1,0:T(8,128)(2,1)S(1)} %fusion.36, s32[8192]{0:T(1024)S(1)} %fusion.58), kind=kCustom, calls=%fused_computation.2 | custom fusion | bytes 33587200 | tf_op jit(solution)/shard_map/gather | solution.py:67
  82.6 13.8 %copy.33 = bf16[16,2,256,1024]{3,2,0,1:T(8,128)(2,1)} copy(bf16[16,2,256,1024]{3,2,1,0:T(8,128)(2,1)} %bitcast.129) | data formatting | bytes 33554432 | tf_op jit(solution)/shard_map/reshape | solution.py:67
  96.4 11.2 %all-to-all-start = ((bf16[16,2,256,1024]{3,2,0,1:T(8,128)(2,1)}), bf16[16,2,256,1024]{3,2,0,1:T(8,128)(2,1)}, u32[]{:S(2)}, u32[]{:S(2)}) async-start(bf16[16,2,256,1024]{3,2,0,1:T(8,128)(2,1)} %copy.33), calls=%async_computation | async-start | bytes 33554432 | tf_op jit(solution)/shard_map/all_to_all | solution.py:68
  108.9 33.0 %gather_fusion.4 = f32[4096]{0:T(1024)S(1)} fusion(f32[512,32]{0,1:T(8,128)S(1)} %fusion.54, s32[4096]{0:T(1024)S(1)} %reshape.430), kind=kCustom, calls=%fused_computation.clone | custom fusion | bytes 65536 | tf_op jit(solution)/shard_map/jit(take_along_axis)/gather | solution.py:17
  143.0 9.2 %reduce-window.16 = s32[32,32,128]{2,1,0:T(8,128)S(1)} reduce-window(s32[32,32,128]{2,1,0:T(8,128)S(1)} %fusion.47, s32[]{:T(128)} %constant.87.clone.1), window={size=1x1x128 pad=0_0x0_0x127_0}, to_apply=%region_11.13 | reduce-window | flops 16646144 | bytes 1048580 | tf_op jit(solution)/shard_map/reduce-window.2
  153.9 16.0 %scatter_custom_fusion.1 = s32[8192]{0:T(1024)S(1)} fusion(s32[4096]{0:T(1024)S(1)} %bitcast.144, s32[4096]{0:T(1024)S(1)} %add_select_fusion, s32[]{:T(128)} %constant.87.clone.1), kind=kCustom, calls=%fused_computation.105 | custom fusion | bytes 32772 | tf_op jit(solution)/shard_map/scatter | solution.py:32
  170.0 13.8 %copy.34 = bf16[16,2,256,1024]{3,2,1,0:T(8,128)(2,1)} copy(bf16[16,2,256,1024]{3,2,0,1:T(8,128)(2,1)} %all-to-all-done) | data formatting | bytes 33554432 | tf_op jit(solution)/shard_map/all_to_all | solution.py:68
  185.7 23.4 %copy.38 = bf16[1,16,1024,512]{3,2,1,0:T(8,128)(2,1)} copy(bf16[1,16,1024,512]{2,1,0,3:T(8,128)(2,1)} %all-gather.15.cloned.1.call-done) | data formatting | bytes 33554432 | tf_op jit(solution)/shard_map/all_gather | solution.py:70
  209.0 14.6 %all-gather.13.cloned.1.call-done = bf16[1,16,1024,512]{2,1,0,3:T(8,128)(2,1)} async-done(((bf16[1,16,1024,8]{2,1,0,3:T(8,128)(2,1)}), bf16[1,16,1024,512]{2,1,0,3:T(8,128)(2,1)}) %all-gather.13.cloned.1.call-update) | async-done | bytes 16777232 | tf_op jit(solution)/shard_map/all_gather | solution.py:69
  223.6 23.3 %copy.36 = bf16[1,16,1024,512]{3,2,1,0:T(8,128)(2,1)} copy(bf16[1,16,1024,512]{2,1,0,3:T(8,128)(2,1)} %all-gather.13.cloned.1.call-done) | data formatting | bytes 33554432 | tf_op jit(solution)/shard_map/all_gather | solution.py:69
  247.0 20.5 %fusion.10 = f32[16,512,512]{2,1,0:T(8,128)} fusion(bf16[16,512,1024]{2,1,0:T(8,128)(2,1)} %bitcast.130, bf16[1,16,1024,512]{3,2,1,0:T(8,128)(2,1)} %copy.38), kind=kOutput, calls=%fused_computation.20 | convolution fusion | flops 8589934592 | bytes 50331648 | tf_op jit(solution)/shard_map/erd,edf->erf/dot_general | solution.py:38
  267.5 68.6 %all-gather.17.cloned.1.call-done = bf16[1,16,512,1024]{3,2,1,0:T(8,128)(2,1)} async-done(((bf16[1,16,8,1024]{3,2,1,0:T(8,128)(2,1)}), bf16[1,16,512,1024]{3,2,1,0:T(8,128)(2,1)}) %all-gather.17.cloned.1.call-update) | async-done | bytes 16777232 | tf_op jit(solution)/shard_map/all_gather | solution.py:71
  336.0 31.2 %fusion.22 = bf16[16,512,1024]{2,1,0:T(8,128)(2,1)} fusion(bf16[1,16,512,1024]{3,2,1,0:T(8,128)(2,1)} %all-gather.17.cloned.1.call-done, f32[16,512,512]{2,1,0:T(8,128)} %fusion.10, bf16[16,512,1024]{2,1,0:T(8,128)(2,1)} %bitcast.131, bf16[1,16,1024,512]{3,2,1,0:T(8,128)(2,1)} %copy.36), kind=kOutput, calls=%fused_computation.26 | convolution fusion | flops 17213423616 | bytes 83886080 | tf_op jit(solution)/shard_map/erf,efd->erd/dot_general | solution.py:40
  367.3 8.2 %copy.39 = bf16[16,2,256,1024]{3,2,0,1:T(8,128)(2,1)S(1)} copy(bf16[16,2,256,1024]{3,2,1,0:T(8,128)(2,1)} %bitcast.134) | data formatting | bytes 33554432 | tf_op jit(solution)/shard_map/reshape | solution.py:73
  375.5 18.1 %all_to_all.20 = bf16[16,2,256,1024]{3,2,0,1:T(8,128)(2,1)S(1)} all-to-all(bf16[16,2,256,1024]{3,2,0,1:T(8,128)(2,1)S(1)} %copy.39), channel_id=1, replica_groups=mesh['rep'=1,'ep'=2,'fsdp'=64] {'ep'}, dimensions={1} | all-to-all | bytes 33554432 | tf_op jit(solution)/shard_map/all_to_all | solution.py:73
  400.2 28.9 %gather_fusion.1 = bf16[4096,1024]{1,0:T(8,128)(2,1)} fusion(bf16[8192,1024]{1,0:T(8,128)(2,1)} %bitcast.126, s32[4096]{0:T(1024)S(1)} %broadcast_clamp_fusion.1), kind=kCustom, calls=%fused_computation.3 | custom fusion | bytes 16793600 | tf_op jit(solution)/shard_map/gather | solution.py:74
  429.1 8.5 %fusion.1 = f32[512,1024]{1,0:T(8,128)S(1)} fusion(bf16[4096,1024]{1,0:T(8,128)(2,1)} %gather_fusion.1, f32[512,8]{1,0:T(8,128)S(1)} %fusion.48), kind=kLoop, calls=%fused_computation.11 | loop fusion | flops 12058624 | bytes 10502144 | tf_op jit(solution)/shard_map/reduce_sum | solution.py:44
  440.4 33.0 %gather_fusion.5 = f32[4096]{0:T(1024)S(1)} fusion(f32[512,32]{0,1:T(8,128)S(1)} %fusion.52, s32[4096]{0:T(1024)S(1)} %copy-done), kind=kCustom, calls=%fused_computation.1.clone | custom fusion | bytes 65536 | tf_op jit(solution)/shard_map/jit(take_along_axis)/gather | solution.py:17
  473.6 35.4 %gather_fusion.2 = bf16[8192,1024]{1,0:T(8,128)(2,1)} fusion(bf16[512,1024]{1,0:T(8,128)(2,1)S(1)} %fusion.40, s32[8192]{0:T(1024)S(1)} %copy-done.6), kind=kCustom, calls=%fused_computation.4 | custom fusion | bytes 33587200 | tf_op jit(solution)/shard_map/gather | solution.py:67
  509.0 8.2 %copy.42 = bf16[16,2,256,1024]{3,2,0,1:T(8,128)(2,1)S(1)} copy(bf16[16,2,256,1024]{3,2,1,0:T(8,128)(2,1)} %bitcast.128) | data formatting | bytes 33554432 | tf_op jit(solution)/shard_map/reshape | solution.py:67
  517.2 17.5 %all_to_all.21 = bf16[16,2,256,1024]{3,2,0,1:T(8,128)(2,1)S(1)} all-to-all(bf16[16,2,256,1024]{3,2,0,1:T(8,128)(2,1)S(1)} %copy.42), channel_id=1, replica_groups=mesh['rep'=1,'ep'=2,'fsdp'=64] {'ep'}, dimensions={1} | all-to-all | bytes 33554432 | tf_op jit(solution)/shard_map/all_to_all | solution.py:68
  541.4 23.3 %copy.47 = bf16[1,16,1024,512]{3,2,1,0:T(8,128)(2,1)} copy(bf16[1,16,1024,512]{2,1,0,3:T(8,128)(2,1)} %all-gather.21.cloned.1.call-done) | data formatting | bytes 33554432 | tf_op jit(solution)/shard_map/all_gather | solution.py:70
  564.7 23.5 %copy.45 = bf16[1,16,1024,512]{3,2,1,0:T(8,128)(2,1)} copy(bf16[1,16,1024,512]{2,1,0,3:T(8,128)(2,1)} %all-gather.19.cloned.1.call-done) | data formatting | bytes 33554432 | tf_op jit(solution)/shard_map/all_gather | solution.py:69
  588.8 20.4 %fusion.4 = f32[16,512,512]{2,1,0:T(8,128)} fusion(bf16[16,512,1024]{2,1,0:T(8,128)(2,1)} %bitcast.132, bf16[1,16,1024,512]{3,2,1,0:T(8,128)(2,1)} %copy.47), kind=kOutput, calls=%fused_computation.14 | convolution fusion | flops 8589934592 | bytes 50331648 | tf_op jit(solution)/shard_map/erd,edf->erf/dot_general | solution.py:38
  609.3 51.6 %all-gather.23.cloned.1.call-done = bf16[1,16,512,1024]{3,2,1,0:T(8,128)(2,1)} async-done(((bf16[1,16,8,1024]{3,2,1,0:T(8,128)(2,1)}), bf16[1,16,512,1024]{3,2,1,0:T(8,128)(2,1)}) %all-gather.23.cloned.1.call-update) | async-done | bytes 16777232 | tf_op jit(solution)/shard_map/all_gather | solution.py:71
  660.8 31.3 %fusion.27 = bf16[16,512,1024]{2,1,0:T(8,128)(2,1)} fusion(bf16[1,16,512,1024]{3,2,1,0:T(8,128)(2,1)} %all-gather.23.cloned.1.call-done, f32[16,512,512]{2,1,0:T(8,128)} %fusion.4, bf16[16,512,1024]{2,1,0:T(8,128)(2,1)} %bitcast.133, bf16[1,16,1024,512]{3,2,1,0:T(8,128)(2,1)} %copy.45), kind=kOutput, calls=%fused_computation.27 | convolution fusion | flops 17213423616 | bytes 83886080 | tf_op jit(solution)/shard_map/erf,efd->erd/dot_general | solution.py:40
  692.1 8.2 %copy.48 = bf16[16,2,256,1024]{3,2,0,1:T(8,128)(2,1)S(1)} copy(bf16[16,2,256,1024]{3,2,1,0:T(8,128)(2,1)} %bitcast.135) | data formatting | bytes 33554432 | tf_op jit(solution)/shard_map/reshape | solution.py:73
  700.3 18.1 %all_to_all.22 = bf16[16,2,256,1024]{3,2,0,1:T(8,128)(2,1)S(1)} all-to-all(bf16[16,2,256,1024]{3,2,0,1:T(8,128)(2,1)S(1)} %copy.48), channel_id=1, replica_groups=mesh['rep'=1,'ep'=2,'fsdp'=64] {'ep'}, dimensions={1} | all-to-all | bytes 33554432 | tf_op jit(solution)/shard_map/all_to_all | solution.py:73
  725.2 28.9 %gather_fusion.3 = bf16[4096,1024]{1,0:T(8,128)(2,1)} fusion(bf16[8192,1024]{1,0:T(8,128)(2,1)} %bitcast.127, s32[4096]{0:T(1024)S(1)} %copy-done.9), kind=kCustom, calls=%fused_computation.5 | custom fusion | bytes 16793600 | tf_op jit(solution)/shard_map/gather | solution.py:74
  754.1 8.5 %fusion = f32[512,1024]{1,0:T(8,128)S(1)} fusion(bf16[4096,1024]{1,0:T(8,128)(2,1)} %gather_fusion.3, f32[512,8]{1,0:T(8,128)S(1)} %fusion.50), kind=kLoop, calls=%fused_computation.9 | loop fusion | flops 12058624 | bytes 10502144 | tf_op jit(solution)/shard_map/reduce_sum | solution.py:44
  (94 shorter events, 46.3 us)
Async XLA Ops:
  6.5 179.1 %all-gather.15.cloned.1.call-start = ((), (), s32[]{:S(2)}) async-start(), calls=%async_computation.5 | async-start | bytes 17039360 | tf_op jit(solution)/shard_map/all_gather | solution.py:70
  8.5 215.2 %all-gather.13.cloned.1.call-start = ((), (), s32[]{:S(2)}) async-start(), calls=%async_computation.4 | async-start | bytes 17039360 | tf_op jit(solution)/shard_map/all_gather | solution.py:69
  10.5 325.5 %all-gather.17.cloned.1.call-start = ((), (), s32[]{:S(2)}) async-start(), calls=%async_computation.6 | async-start | bytes 17039360 | tf_op jit(solution)/shard_map/all_gather | solution.py:71
  12.4 529.0 %all-gather.21.cloned.1.call-start = ((), (), s32[]{:S(2)}) async-start(), calls=%async_computation.8 | async-start | bytes 17039360 | tf_op jit(solution)/shard_map/all_gather | solution.py:70
  13.4 551.4 %all-gather.19.cloned.1.call-start = ((), (), s32[]{:S(2)}) async-start(), calls=%async_computation.7 | async-start | bytes 17039360 | tf_op jit(solution)/shard_map/all_gather | solution.py:69
  14.3 646.5 %all-gather.23.cloned.1.call-start = ((), (), s32[]{:S(2)}) async-start(), calls=%async_computation.9 | async-start | bytes 17039360 | tf_op jit(solution)/shard_map/all_gather | solution.py:71
  96.4 12.1 %copy-start.7 = (bf16[2,1024,32]{1,2,0:T(8,128)(2,1)S(1)}, bf16[2,1024,32]{1,2,0:T(8,128)(2,1)}, u32[]{:S(2)}) copy-start(bf16[2,1024,32]{1,2,0:T(8,128)(2,1)} %param.11) | copy-start | bytes 393220
  96.4 73.6 %all-to-all-start = ((bf16[16,2,256,1024]{3,2,0,1:T(8,128)(2,1)}), bf16[16,2,256,1024]{3,2,0,1:T(8,128)(2,1)}, u32[]{:S(2)}, u32[]{:S(2)}) async-start(bf16[16,2,256,1024]{3,2,0,1:T(8,128)(2,1)} %copy.33), calls=%async_computation | async-start | bytes 33554432 | tf_op jit(solution)/shard_map/all_to_all | solution.py:68
  107.7 34.4 %copy-start.1 = (s32[1,512,8]{2,1,0:T(8,128)}, s32[1,512,8]{2,1,0:T(8,128)S(1)}, u32[]{:S(2)}) copy-start(s32[1,512,8]{2,1,0:T(8,128)S(1)} %copy.53) | copy-start | bytes 49156
  400.2 37.4 %copy-start.3 = (bf16[512,1024]{1,0:T(8,128)(2,1)S(1)}, bf16[512,1024]{1,0:T(8,128)(2,1)}, u32[]{:S(2)}) copy-start(bf16[512,1024]{1,0:T(8,128)(2,1)} %param.9) | copy-start | bytes 3145732
  429.1 10.9 %copy-start.8 = (bf16[2,1024,32]{1,2,0:T(8,128)(2,1)S(1)}, bf16[2,1024,32]{1,2,0:T(8,128)(2,1)}, u32[]{:S(2)}) copy-start(bf16[2,1024,32]{1,2,0:T(8,128)(2,1)} %param.11) | copy-start | bytes 393220
  429.1 11.3 %copy-start = (s32[4096]{0:T(1024)S(1)}, s32[4096]{0:T(1024)}, u32[]{:S(2)}) copy-start(s32[4096]{0:T(1024)} %reshape.435) | copy-start | bytes 49156
  438.0 1.0 copy-start.4
  440.4 33.2 %copy-start.6 = (s32[8192]{0:T(1024)S(1)}, s32[8192]{0:T(1024)}, u32[]{:S(2)}) copy-start(s32[8192]{0:T(1024)} %fusion.59) | copy-start | bytes 98308
  564.7 23.5 %copy-start.2 = (s32[1,512,8]{2,1,0:T(8,128)S(1)}, s32[1,512,8]{2,1,0:T(8,128)}, u32[]{:S(2)}) copy-start(s32[1,512,8]{2,1,0:T(8,128)} %copy-done.1) | copy-start | bytes 49156
  718.5 6.7 copy-start.9
  725.2 37.4 %copy-start.5 = (bf16[512,1024]{1,0:T(8,128)(2,1)S(1)}, bf16[512,1024]{1,0:T(8,128)(2,1)}, u32[]{:S(2)}) copy-start(bf16[512,1024]{1,0:T(8,128)(2,1)} %copy-done.4) | copy-start | bytes 3145732
Sparse Core Ops, SparseCore 0:
  10.2 106.9 all-gather.14
  120.1 103.5 all-gather.12
  226.6 109.4 all-gather.16
  338.8 103.4 all-gather.20
  445.1 103.4 all-gather.18
  551.4 109.4 all-gather.22
where the time goes:
time: 782 us; the launch traced here: 771 us
  local copies, waits for them, and re-layouts  406 us (52%)
  waiting for transfers between devices  135 us (17%)
  matrix products  104 us (13%)
  blocking collectives  53.7 us (7%)
  other arithmetic  45.7 us (6%)
  between operations  14.3 us (2%)
  starting transfers between devices  11.4 us (1%)
    all_gather x2, waiting for transfers between devices, device_step(): down_full = lax.all_gather(down_w[layer_idx], 'fsdp', axis=1, tiled=True)  120 us
    gather x2, local copies, waits for them, and re-layouts, device_step(): send_buf = hidden[slot_token].reshape(n_local, owners, capacity, d_model)  70.7 us
    gather x6, local copies, waits for them, and re-layouts, route_gates(): jnp.take_along_axis(logits, routes_l, axis=-1)  67.3 us
    dot_general x2, matrix products, expert_ffn(): jnp.einsum('erf,efd->erd', inner_act, down_full, preferred_element_type=j...  62.6 us
    gather x2, local copies, waits for them, and re-layouts, device_step(): back_buf.reshape(experts * capacity, d_model)[pair_slot]  57.8 us
    all_gather x2, local copies, waits for them, and re-layouts, device_step(): gate_full = lax.all_gather(gate_w[layer_idx], 'fsdp', axis=2, tiled=True)  46.8 us
    all_gather x2, local copies, waits for them, and re-layouts, device_step(): up_full = lax.all_gather(up_w[layer_idx], 'fsdp', axis=2, tiled=True)  46.7 us
    dot_general x2, matrix products, expert_ffn(): jnp.einsum('erd,edf->erf', expert_rows, up_full, preferred_element_type=j...  40.9 us
  transfers between devices with their start and end apart: 7, of which 3 were waited for; matrix products, arithmetic and copies ran while one was open for 61% of the time, Pallas kernels for 0%

commit v1 on v0

v1 whole, which is shorter than its diff:
```python
import functools

import jax
import jax.numpy as jnp
from jax import lax
from jax.experimental import pallas as pl
from jax.experimental.pallas import tpu as pltpu
from jax.sharding import Mesh, PartitionSpec as P

NORM_EPS = 1e-5
MESH_ID = pl.DeviceIdType.MESH

O_A, O_B, R_B, L_A, R_A, L_B, F_A, F_B = range(8)
UNITS = 8


def rms_norm(stream, norm_row):
    widened = stream.astype(jnp.float32)
    inv_rms = lax.rsqrt(jnp.mean(widened * widened, axis=-1, keepdims=True) + NORM_EPS)
    return (widened * inv_rms * norm_row).astype(jnp.bfloat16)


def dense_gates(hidden, router_l, routes_l):
    experts = router_l.shape[1]
    logits = jnp.dot(hidden, router_l, preferred_element_type=jnp.float32)
    ids = jnp.arange(experts, dtype=routes_l.dtype)
    chosen = jnp.any(routes_l[:, :, None] == ids[None, None, :], axis=1)
    top = jnp.max(jnp.where(chosen, logits, -jnp.inf), axis=-1, keepdims=True)
    weight = jnp.where(chosen, jnp.exp(jnp.where(chosen, logits - top, 0.0)), 0.0)
    gates = weight / jnp.sum(weight, axis=-1, keepdims=True)
    return jnp.where(chosen, gates, -1.0).T


def layer_kernel(h_ref, g_ref, w_ref, x_ref, out_ref, h_all, g_all, w_v, acc, pair_in, ring_in,
                 own_sem, w_sem, ag_send, ag_recv, agp_send, agp_recv, pair_send, pair_recv, ring_send, ring_recv):
    half, d_model = h_all.shape[1] // 2, h_all.shape[2]
    n_exp = w_v.shape[0]
    ep, x = lax.axis_index("ep"), lax.axis_index("x")
    n_x = 4
    right = {"x": lax.rem(x + 1, n_x)}
    left = {"x": lax.rem(x + n_x - 1, n_x)}
    partner = {"ep": 1 - ep}
    group = ep * n_x + x

    barrier = pltpu.get_barrier_semaphore()
    for peer in (right, left, partner):
        pl.semaphore_signal(barrier, inc=1, device_id=peer, device_id_type=MESH_ID)

    own = []
    for unit in (O_A, O_B):
        rows = pl.ds((unit - O_A) * half, half)
        own.append(pltpu.make_async_copy(h_ref.at[rows], h_all.at[unit, pl.ds(0, half)], own_sem.at[2 * unit]))
        own.append(pltpu.make_async_copy(g_ref.at[:, rows], g_all.at[unit, 0], own_sem.at[2 * unit + 1]))
    for copy in own:
        copy.start()
    loads = [pltpu.make_async_copy(w_ref.at[:, e], w_v.at[e], w_sem.at[e]) for e in range(n_exp)]
    for copy in loads:
        copy.start()
    for copy in own:
        copy.wait()
    pl.semaphore_wait(barrier, 3)

    def gather_copy(idx, unit, dst, peer):
        return (
            pltpu.make_async_remote_copy(
                h_all.at[unit, pl.ds(0, half)], h_all.at[dst, pl.ds(0, half)],
                ag_send.at[2 * idx], ag_recv.at[2 * idx], device_id=peer, device_id_type=MESH_ID),
            pltpu.make_async_remote_copy(
                g_all.at[unit, 0], g_all.at[dst, 0],
                ag_send.at[2 * idx + 1], ag_recv.at[2 * idx + 1], device_id=peer, device_id_type=MESH_ID),
        )

    def pair_copy(unit):
        return (
            pltpu.make_async_remote_copy(
                h_all.at[unit, pl.ds(0, half)], h_all.at[unit, pl.ds(half, half)],
                agp_send.at[2 * unit], agp_recv.at[2 * unit], device_id=partner, device_id_type=MESH_ID),
            pltpu.make_async_remote_copy(
                g_all.at[unit, 0], g_all.at[unit, 1],
                agp_send.at[2 * unit + 1], agp_recv.at[2 * unit + 1], device_id=partner, device_id_type=MESH_ID),
        )

    moves = {
        L_A: (0, O_A, right), R_B: (1, O_B, left),
        L_B: (2, O_B, right), R_A: (3, O_A, left),
        F_A: (4, L_A, right), F_B: (5, R_B, left),
    }

    def ring_gather(dst):
        idx, src, peer = moves[dst]
        return gather_copy(idx, src, dst, peer)

    def start(copies):
        for copy in copies:
            copy.start()

    def wait_recv(copies):
        for copy in copies:
            copy.wait_recv()

    def wait_send(copies):
        for copy in copies:
            copy.wait_send()

    def reduce_pair(unit):
        return pltpu.make_async_remote_copy(
            acc.at[unit, pl.ds(half, half)], pair_in.at[unit],
            pair_send.at[unit], pair_recv.at[unit], device_id=partner, device_id_type=MESH_ID)

    sums = {R_B: (0, right), F_A: (1, right), R_A: (2, right), L_A: (3, left), F_B: (4, left), L_B: (5, left)}

    def reduce_ring(unit):
        slot, peer = sums[unit]
        return pltpu.make_async_remote_copy(
            acc.at[unit, pl.ds(0, half)], ring_in.at[slot],
            ring_send.at[slot], ring_recv.at[slot], device_id=peer, device_id_type=MESH_ID)

    def add_pair(unit):
        reduce_pair(unit).wait_recv()
        acc[unit, 0:half, :] += pair_in[unit]

    start(ring_gather(L_A))
    start(ring_gather(R_B))
    for unit in (O_A, O_B):
        start(pair_copy(unit))
    start(ring_gather(L_B))
    start(ring_gather(R_A))

    def at(step, t, action):
        @pl.when(step == t)
        def _():
            action()

    def arrive(*units):
        for unit in units:
            wait_recv(ring_gather(unit))
            if unit == L_A:
                start(ring_gather(F_A))
            if unit == R_B:
                start(ring_gather(F_B))
            start(pair_copy(unit))

    def step_fn(step, carry):
        unit, e = step // n_exp, step % n_exp
        for first_use, load in enumerate(loads):
            at(step, first_use, load.wait)
        at(step, 7, lambda: arrive(L_A, R_B))
        at(step, 14, lambda: arrive(L_B, R_A))
        at(step, 22, lambda: arrive(F_A, F_B))
        for k in range(UNITS):
            at(step, n_exp * k, lambda: wait_recv(pair_copy(k)))
            if k < UNITS - 1:
                at(step, n_exp * (k + 1), lambda: reduce_pair(k).start())
                if n_exp * (k + 1) + 2 < n_exp * UNITS:
                    at(step, n_exp * (k + 1) + 2, lambda: add_pair(k))
                    if k in (R_B, L_A, F_A):
                        at(step, n_exp * (k + 1) + 3, lambda: reduce_ring(k).start())

        tokens = h_all[unit]
        gate_w = w_v[e, :, 0].reshape(-1, d_model)
        up_w = w_v[e, :, 1].reshape(-1, d_model)
        down_w = w_v[e, :, 2].reshape(-1, d_model)
        d_ff = gate_w.shape[0]
        inner = []
        for f in range(0, d_ff, 256):
            nt = (((1,), (1,)), ((), ()))
            u = lax.dot_general(tokens, gate_w[f:f + 256], nt, preferred_element_type=jnp.float32)
            v = lax.dot_general(tokens, up_w[f:f + 256], nt, preferred_element_type=jnp.float32)
            inner.append((jax.nn.silu(u) * v).astype(jnp.bfloat16))
        inner = jnp.concatenate(inner, axis=1)
        row = group * n_exp + e
        gate_cols = []
        for s in range(2):
            gates = g_all[unit, s, pl.ds(row, 1), :]
            gate_cols.append(jnp.broadcast_to(gates, (128, half)).T)
        gate_b = jnp.concatenate(gate_cols, axis=0)
        gate_b = jnp.concatenate([gate_b, gate_b], axis=1)
        first = e == 0
        for c in range(0, d_model, 256):
            o = jnp.dot(inner, down_w[:, c:c + 256], preferred_element_type=jnp.float32)
            o = o.astype(jnp.bfloat16).astype(jnp.float32)
            part = jnp.where(gate_b >= 0.0, gate_b * o, 0.0)
            prev = jnp.where(first, 0.0, acc[unit, :, c:c + 256])
            acc[unit, :, c:c + 256] = prev + part
        return carry

    lax.fori_loop(0, UNITS * n_exp, step_fn, 0)

    last = UNITS - 1
    reduce_pair(last).start()
    for unit in (last,):
        add_pair(unit)
        reduce_ring(unit).start()
    reduce_ring(F_A).wait_recv()
    acc[R_A, 0:half, :] += ring_in[1]
    reduce_ring(R_A).start()
    reduce_ring(F_B).wait_recv()
    acc[L_B, 0:half, :] += ring_in[4]
    reduce_ring(L_B).start()

    reduce_ring(R_B).wait_recv()
    reduce_ring(L_A).wait_recv()
    acc[O_B, 0:half, :] += x_ref[half:, :].astype(jnp.float32) + ring_in[0]
    acc[O_A, 0:half, :] += x_ref[:half, :].astype(jnp.float32) + ring_in[3]
    reduce_ring(R_A).wait_recv()
    out_ref[0:half, :] = (acc[O_A, 0:half, :] + ring_in[2]).astype(out_ref.dtype)
    reduce_ring(L_B).wait_recv()
    out_ref[half:, :] = (acc[O_B, 0:half, :] + ring_in[5]).astype(out_ref.dtype)

    for unit in range(UNITS):
        wait_send(pair_copy(unit))
        reduce_pair(unit).wait_send()
        if unit in moves:
            wait_send(ring_gather(unit))
        if unit in sums:
            reduce_ring(unit).wait_send()


def moe_layer(idx, hidden, gates, weights, stream):
    tok_dev, d_model = hidden.shape
    half = tok_dev // 2
    n_exp = weights.shape[1]
    vmem = pl.BlockSpec(memory_space=pltpu.VMEM)
    hbm = pl.BlockSpec(memory_space=pl.ANY)
    dma = pltpu.SemaphoreType.DMA
    return pl.pallas_call(
        layer_kernel,
        name="moe_layer",
        out_shape=jax.ShapeDtypeStruct(stream.shape, stream.dtype),
        in_specs=[hbm, hbm, hbm, vmem],
        out_specs=vmem,
        scratch_shapes=[
            pltpu.VMEM((UNITS, tok_dev, d_model), jnp.bfloat16),
            pltpu.VMEM((UNITS, 2, gates.shape[0], half), jnp.float32),
            pltpu.VMEM((n_exp, weights.shape[0]) + weights.shape[2:], jnp.bfloat16),
            pltpu.VMEM((UNITS, tok_dev, d_model), jnp.float32),
            pltpu.VMEM((UNITS, half, d_model), jnp.float32),
            pltpu.VMEM((6, half, d_model), jnp.float32),
            dma((4,)), dma((n_exp,)),
            dma((12,)), dma((12,)), dma((16,)), dma((16,)), dma((8,)), dma((8,)), dma((6,)), dma((6,)),
        ],
        compiler_params=pltpu.CompilerParams(
            collective_id=0, has_side_effects=True, vmem_limit_bytes=67043328),
        cost_estimate=pl.CostEstimate(flops=52 * 10**9, bytes_accessed=16 * 2**20, transcendentals=0),
    )(hidden, gates, weights, stream)


def solution(mesh):
    n_x = 4
    n_y = min(4, mesh.shape["fsdp"] // n_x)
    devices = mesh.devices.reshape(mesh.shape["rep"], mesh.shape["ep"], -1, n_y, n_x)
    cells = Mesh(devices, ("rep", "ep", "z", "y", "x"))
    fsdp = ("z", "y", "x")
    token_spec = P(("rep", "ep") + fsdp, None)
    expert_in_spec = P(None, "ep", None, fsdp)
    expert_out_spec = P(None, "ep", fsdp, None)
    route_spec = P(None, ("rep", "ep") + fsdp, None)

    def device_step(x_in, norm_w, router_w, gate_w, up_w, down_w, routes):
        layers = routes.shape[0]
        n_local = gate_w.shape[1]
        n_exp = n_local // n_x
        f_dev = gate_w.shape[3]
        d_model = x_in.shape[1]

        stacked = jnp.stack([gate_w.transpose(0, 1, 3, 2), up_w.transpose(0, 1, 3, 2), down_w], axis=2)
        stacked = stacked.reshape(layers, n_x, n_exp, 3, f_dev, d_model)
        swapped = lax.all_to_all(stacked, "x", 1, 1, tiled=True)
        swapped = swapped.transpose(0, 2, 3, 1, 4, 5).reshape(layers, 1, n_exp, 3, n_x * f_dev, d_model)
        full = [lax.all_gather(swapped[l], ("z", "y"), axis=0, tiled=True) for l in range(layers)]

        stream = x_in
        for l in range(layers):
            hidden = rms_norm(stream, norm_w[l])
            gates = dense_gates(hidden, router_w[l], routes[l])
            stream = moe_layer(l, hidden, gates, full[l], stream)
        return stream

    return jax.shard_map(device_step, mesh=cells,
                         in_specs=(token_spec, P(), P(), expert_in_spec, expert_in_spec, expert_out_spec, route_spec),
                         out_specs=token_spec, check_vma=False)
```

time: 782 us -> 399 us (0.51); the launches traced: 771 us -> 399 us
  local copies, waits for them, and re-layouts: 406 us -> 6.54 us
  Pallas kernels: 0 us -> 259 us
  matrix products: 104 us -> 0.87 us
  waiting for transfers between devices: 135 us -> 87.3 us
  other arithmetic: 45.7 us -> 7.31 us
  blocking collectives: 53.7 us -> 24.5 us
  starting transfers between devices: 11.4 us -> 0.04 us
    pallas_call x0 -> x2, Pallas kernels: none -> 259 us  [moe_layer(): pl.pallas_call(layer_kernel, name='moe_layer', out_shape=jax.ShapeDtypeSt...]
    gather x10 -> x0, local copies, waits for them, and re-layouts: 196 us -> none  [the longest x2 70.7 us: device_step(): send_buf = hidden[slot_token].reshape(n_local, owners, capacity, d_model)]
    dot_general x6 -> x2, matrix products: 104 us -> 0.87 us  [dense_gates(): logits = jnp.dot(hidden, router_l, preferred_element_type=jnp.float32)]
    all_gather x4 -> x0, local copies, waits for them, and re-layouts: 93.6 us -> none  [the longest x2 46.8 us: device_step(): gate_full = lax.all_gather(gate_w[layer_idx], 'fsdp', axis=2, tiled=True)]
    all_gather x6 -> x2, waiting for transfers between devices: 135 us -> 86.6 us  [device_step(): lax.all_gather(swapped[l], ('z', 'y'), axis=0, tiled=True)]
    reshape x4 -> x0, local copies, waits for them, and re-layouts: 38.4 us -> none  [the longest x2 22 us: device_step(): send_buf = hidden[slot_token].reshape(n_local, owners, capacity, d_model)]
    all_to_all x4 -> x1, local copies, waits for them, and re-layouts: 33.8 us -> 0.16 us  [device_step(): swapped = lax.all_to_all(stacked, 'x', 1, 1, tiled=True)]
    scatter x2 -> x0, local copies, waits for them, and re-layouts: 31.6 us -> none  [slot_plan(): jnp.zeros((experts * capacity,), jnp.int32).at[pair_slot].set(pair_token)]
  transfers between devices with their start and end apart: 7 -> 2, of which waited for: 3 -> 1; matrix products, arithmetic and copies ran while one was open for 61% -> 2% of each run, Pallas kernels for 0% -> 33%
where the time goes in v1:
time: 399 us
  Pallas kernels  259 us (65%)
  waiting for transfers between devices  87.3 us (22%)
  blocking collectives  24.5 us (6%)
  between operations  13.6 us (3%)
  other arithmetic  7.31 us (2%)
  local copies, waits for them, and re-layouts  6.54 us (2%)
    pallas_call x2, Pallas kernels, moe_layer(): pl.pallas_call(layer_kernel, name='moe_layer', out_shape=jax.ShapeDtypeSt...  259 us
    all_gather x2, waiting for transfers between devices, device_step(): lax.all_gather(swapped[l], ('z', 'y'), axis=0, tiled=True)  86.6 us
    all_to_all x1, blocking collectives, device_step(): swapped = lax.all_to_all(stacked, 'x', 1, 1, tiled=True)  24.5 us
  transfers between devices with their start and end apart: 2, of which 1 were waited for; matrix products, arithmetic and copies ran while one was open for 2% of the time, Pallas kernels for 33%

profile of v1, /device:TPU:1, one launch (start us, length us, event | category | flops | bytes accessed | tf_op | source)
XLA Modules:
  0.0 398.7 jit_solution(18018898450380207880)
XLA Ops:
  6.5 0.0 all-gather.3.cloned.1.call-start
  6.5 1.5 pad_maximum_fusion
  8.1 0.2 copy.19
  8.2 24.5 %all_to_all.5 = bf16[2,4,4,3,8,1024]{5,4,3,2,0,1:T(8,128)(2,1)S(1)} all-to-all(bf16[2,4,4,3,8,1024]{5,4,3,2,0,1:T(8,128)(2,1)S(1)} %copy.19), channel_id=1, replica_groups=mesh['rep'=1,'ep'=2,'z'=4,'y'=4,'x'=4] {'x'}, dimensions={1} | all-to-all | bytes 3145728 | tf_op jit(solution)/shard_map/all_to_all | solution.py:268
  32.8 0.2 copy.22
  32.9 0.0 copy-start.6
  32.9 0.0 copy-start.2
  32.9 1.4 slice_bitcast_fusion
  34.3 0.0 all-gather.3.cloned.1.call-update
  34.4 0.0 copy-start.4
  34.4 0.0 all-gather.5.cloned.1.call-start
  34.4 0.7 all-gather.5.cloned.1.call-update
  35.1 0.1 fusion.6
  35.2 0.3 fusion
  35.5 0.6 fusion.22
  36.1 0.3 fusion.2.h_ref
  36.4 0.0 copy-start
  36.5 1.0 copy-done
  37.4 0.4 select_reduce_fusion.3
  37.9 0.7 fusion.7
  38.6 0.6 fusion.17.g_ref
  39.2 86.6 %all-gather.3.cloned.1.call-done.w_ref = bf16[16,4,3,32,1024]{4,3,2,1,0:T(8,128)(2,1)} async-done(((bf16[1,4,3,32,1024]{4,3,2,1,0:T(8,128)(2,1)}), bf16[16,4,3,32,1024]{4,3,2,1,0:T(8,128)(2,1)}) %all-gather.3.cloned.1.call-update) | async-done | bytes 12582928 | tf_op jit(solution)/shard_map/all_gather | solution.py:270
  125.8 129.7 %moe_layer.2.x_ref = bf16[512,1024]{1,0:T(8,128)(2,1)} custom-call(bf16[512,1024]{1,0:T(8,128)(2,1)} %copy-done, f32[32,512]{1,0:T(8,128)} %fusion.17.g_ref, bf16[16,4,3,32,1024]{4,3,2,1,0:T(8,128)(2,1)} %all-gather.3.cloned.1.call-done.w_ref, bf16[512,1024]{1,0:T(8,128)(2,1)} %x_ref.1), custom_call_target="tpu_custom_call" | custom-call | flops 51999997952 | bytes 16777216 | tf_op jit(solution)/shard_map/moe_layer/pallas_call | solution.py:226
  255.5 0.0 copy-start.5
  255.5 1.5 fusion.3
  257.1 1.5 fusion.5.h_ref
  258.6 0.0 copy-start.1
  258.6 1.0 copy-done.1
  259.6 0.4 select_reduce_fusion.1
  260.1 0.6 fusion.11.g_ref
  260.7 128.8 %moe_layer.3 = bf16[512,1024]{1,0:T(8,128)(2,1)} custom-call(bf16[512,1024]{1,0:T(8,128)(2,1)} %copy-done.1, f32[32,512]{1,0:T(8,128)} %fusion.11.g_ref, bf16[16,4,3,32,1024]{4,3,2,1,0:T(8,128)(2,1)} %all-gather.5.cloned.1.call-done.w_ref, bf16[512,1024]{1,0:T(8,128)(2,1)} %moe_layer.2.x_ref), custom_call_target="tpu_custom_call" | custom-call | flops 51999997952 | bytes 16777216 | tf_op jit(solution)/shard_map/moe_layer/pallas_call | solution.py:226
  389.6 2.3 copy.24
  (14 shorter events, 0.1 us)
Async XLA Ops:
  6.5 119.2 %all-gather.3.cloned.1.call-start = ((), (), s32[]{:S(2)}) async-start(), calls=%async_computation.1 | async-start | bytes 13369344 | tf_op jit(solution)/shard_map/all_gather | solution.py:270
  32.9 2.2 copy-start.6
  32.9 2.3 copy-start.2
  34.3 1.2 copy-start.7
  34.4 3.1 copy-start.4
  34.4 226.4 %all-gather.5.cloned.1.call-start = ((), (), s32[]{:S(2)}) async-start(), calls=%async_computation.2 | async-start | bytes 13369344 | tf_op jit(solution)/shard_map/all_gather | solution.py:270
  36.4 1.0 copy-start
  255.5 4.1 %copy-start.3 = (pred[512,32]{0,1:T(8,128)(4,1)S(1)}, pred[512,32]{0,1:T(8,128)(4,1)}, u32[]{:S(2)}) copy-start(pred[512,32]{0,1:T(8,128)(4,1)} %fusion.7) | copy-start | bytes 49156
  255.5 4.1 %copy-start.5 = (bf16[2,1024,32]{1,2,0:T(8,128)(2,1)S(1)}, bf16[2,1024,32]{1,2,0:T(8,128)(2,1)}, u32[]{:S(2)}) copy-start(bf16[2,1024,32]{1,2,0:T(8,128)(2,1)} %param.9) | copy-start | bytes 393220
  258.6 1.0 copy-start.1
Sparse Core Ops, SparseCore 0:
  34.5 91.2 all-gather.2
  127.9 89.3 all-gather.4

commit v2 on v1

v2 whole, which is shorter than its diff:
```python
import functools

import jax
import jax.numpy as jnp
from jax import lax
from jax.experimental import pallas as pl
from jax.experimental.pallas import tpu as pltpu
from jax.sharding import Mesh, PartitionSpec as P

NORM_EPS = 1e-5
MESH_ID = pl.DeviceIdType.MESH

O_A, O_B, R_B, L_A, F_A, F_B, R_A, L_B = range(8)
UNITS = 8


def rms_norm(stream, norm_row):
    widened = stream.astype(jnp.float32)
    inv_rms = lax.rsqrt(jnp.mean(widened * widened, axis=-1, keepdims=True) + NORM_EPS)
    return (widened * inv_rms * norm_row).astype(jnp.bfloat16)


def dense_gates(hidden, router_l, routes_l):
    experts = router_l.shape[1]
    logits = jnp.dot(hidden, router_l, preferred_element_type=jnp.float32)
    ids = jnp.arange(experts, dtype=routes_l.dtype)
    chosen = jnp.any(routes_l[:, :, None] == ids[None, None, :], axis=1)
    top = jnp.max(jnp.where(chosen, logits, -jnp.inf), axis=-1, keepdims=True)
    weight = jnp.where(chosen, jnp.exp(jnp.where(chosen, logits - top, 0.0)), 0.0)
    gates = weight / jnp.sum(weight, axis=-1, keepdims=True)
    return jnp.where(chosen, gates, -1.0).T


def layer_kernel(first, ring_shape, *refs):
    if first:
        (h_ref, g_ref, gate_ref, up_ref, down_ref, x_ref, out_ref, next_ref, h_all, g_all, w_v, acc, pair_in, ring_in,
         own_sem, ag_send, ag_recv, agp_send, agp_recv, pair_send, pair_recv, ring_send, ring_recv,
         pre_own, pre_send, pre_recv, wr_send, wr_recv) = refs
    else:
        (h_ref, g_ref, w_ref, x_ref, out_ref, h_all, g_all, w_v, acc, pair_in, ring_in,
         own_sem, ag_send, ag_recv, agp_send, agp_recv, pair_send, pair_recv, ring_send, ring_recv, w_sem) = refs
    half, d_model = h_all.shape[1] // 2, h_all.shape[2]
    n_exp = w_v.shape[0]
    n_z, n_y, n_x = ring_shape
    with_ring = n_z == 4 and n_y == 4
    ep, x = lax.axis_index("ep"), lax.axis_index("x")
    z, y = lax.axis_index("z"), lax.axis_index("y")
    right = {"x": lax.rem(x + 1, n_x)}
    left = {"x": lax.rem(x + n_x - 1, n_x)}
    partner = {"ep": 1 - ep}
    group = ep * n_x + x

    def remote(src, dst, send, recv, peer):
        return pltpu.make_async_remote_copy(src, dst, send, recv, device_id=peer, device_id_type=MESH_ID)

    peers = [right, left, partner]
    if first:
        peers.append({"x": lax.rem(x + 2, n_x)})
        if with_ring:
            for axis, pos in (("z", z), ("y", y)):
                peers += [{axis: lax.rem(pos + 1, 4)}, {axis: lax.rem(pos + 3, 4)}]
    barrier = pltpu.get_barrier_semaphore()
    for peer in peers:
        pl.semaphore_signal(barrier, inc=1, device_id=peer, device_id_type=MESH_ID)

    own = []
    for unit in (O_A, O_B):
        rows = pl.ds((unit - O_A) * half, half)
        own.append(pltpu.make_async_copy(h_ref.at[rows], h_all.at[unit, pl.ds(0, half)], own_sem.at[2 * unit]))
        own.append(pltpu.make_async_copy(g_ref.at[:, rows], g_all.at[unit, 0], own_sem.at[2 * unit + 1]))

    if first:
        sources = (gate_ref, up_ref, down_ref)
        targets = (w_v, next_ref)

        def pre_local(layer, m):
            return pltpu.make_async_copy(
                sources[m].at[layer, pl.ds(x * n_exp, n_exp)], targets[layer].at[:, m, z, y, x],
                pre_own.at[layer * 3 + m])

        def pre_copy(layer, m, k):
            there = lax.rem(x + k, n_x)
            idx = (layer * 3 + m) * 3 + k - 1
            return remote(sources[m].at[layer, pl.ds(there * n_exp, n_exp)], targets[layer].at[:, m, z, y, x],
                          pre_send.at[idx], pre_recv.at[idx], {"x": there})

        def ring_copy(layer, r, m, p):
            buf = targets[layer]
            step = 1 if p % 2 == 0 else -1
            along_z = (r < 3) == (p < 2)
            pos = z if along_z else y
            i = lax.rem(pos + 4 - step * (r % 3), 4)
            if r < 3:
                piece = buf.at[p, m, i, y] if along_z else buf.at[p, m, z, i]
            else:
                piece = buf.at[p, m, i] if along_z else buf.at[p, m, :, i]
            idx = ((layer * 6 + r) * 3 + m) * 4 + p
            peer = {"z" if along_z else "y": lax.rem(pos + 4 + step, 4)}
            return remote(piece, piece, wr_send.at[idx], wr_recv.at[idx], peer)

        def pre_start(layer):
            for m in range(3):
                for k in (1, 3, 2):
                    pre_copy(layer, m, k).start()
                pre_local(layer, m).start()

        def pre_wait(layer, m):
            pre_local(layer, m).wait()
            for k in (1, 3, 2):
                pre_copy(layer, m, k).wait_recv()

        def ring_event(layer, r, m):
            if r == 0:
                pre_wait(layer, m)
            if with_ring:
                for p in range(4):
                    if r > 0:
                        ring_copy(layer, r - 1, m, p).wait_recv()
                    if r < 6:
                        ring_copy(layer, r, m, p).start()

        def ring_round(layer, r):
            for m in range(3):
                ring_event(layer, r, m)
    else:
        loads = [pltpu.make_async_copy(w_ref.at[e], w_v.at[e], w_sem.at[e]) for e in range(n_exp)]

    def pair_copy(unit):
        return (
            remote(h_all.at[unit, pl.ds(0, half)], h_all.at[unit, pl.ds(half, half)],
                   agp_send.at[2 * unit], agp_recv.at[2 * unit], partner),
            remote(g_all.at[unit, 0], g_all.at[unit, 1],
                   agp_send.at[2 * unit + 1], agp_recv.at[2 * unit + 1], partner),
        )

    moves = {
        L_A: (0, O_A, right), R_B: (1, O_B, left),
        L_B: (2, O_B, right), R_A: (3, O_A, left),
        F_A: (4, L_A, right), F_B: (5, R_B, left),
    }

    def ring_gather(dst):
        idx, src, peer = moves[dst]
        return (
            remote(h_all.at[src, pl.ds(0, half)], h_all.at[dst, pl.ds(0, half)],
                   ag_send.at[2 * idx], ag_recv.at[2 * idx], peer),
            remote(g_all.at[src, 0], g_all.at[dst, 0], ag_send.at[2 * idx + 1], ag_recv.at[2 * idx + 1], peer),
        )

    def start(copies):
        for copy in copies:
            copy.start()

    def wait_recv(copies):
        for copy in copies:
            copy.wait_recv()

    def wait_send(copies):
        for copy in copies:
            copy.wait_send()

    def reduce_pair(unit):
        return remote(acc.at[unit, pl.ds(half, half)], pair_in.at[unit],
                      pair_send.at[unit], pair_recv.at[unit], partner)

    sums = {R_B: (0, right), F_A: (1, right), R_A: (2, right), L_A: (3, left), F_B: (4, left), L_B: (5, left)}

    def reduce_ring(unit):
        slot, peer = sums[unit]
        return remote(acc.at[unit, pl.ds(0, half)], ring_in.at[slot], ring_send.at[slot], ring_recv.at[slot], peer)

    def add_pair(unit):
        reduce_pair(unit).wait_recv()
        acc[unit, 0:half, :] += pair_in[unit]

    def add_far(unit, far):
        reduce_ring(far).wait_recv()
        acc[unit, 0:half, :] += ring_in[sums[far][0]]

    def arrive(*units):
        for unit in units:
            wait_recv(ring_gather(unit))
            if unit == L_A:
                start(ring_gather(F_A))
            if unit == R_B:
                start(ring_gather(F_B))
            start(pair_copy(unit))

    for copy in own:
        copy.start()
    if not first:
        start(loads)
    for copy in own:
        copy.wait()
    pl.semaphore_wait(barrier, len(peers))
    if first:
        pre_start(0)
    start(ring_gather(L_A))
    start(ring_gather(R_B))
    for unit in (O_A, O_B):
        start(pair_copy(unit))
    if first:
        start(ring_gather(L_B))
        start(ring_gather(R_A))

    plan = {}

    def at(t, action, *args):
        plan.setdefault(t, []).append((action, args))

    if first:
        order = (F_A, F_B, R_B, L_A, R_A, L_B, O_A, O_B)
        for r in range(3):
            ring_round(0, r)
        arrive(L_A, R_B)
        pre_start(1)
        ring_round(0, 3)
        ring_round(0, 4)
        arrive(L_B, R_A)
        ring_round(0, 5)
        arrive(F_A, F_B)
        ring_round(1, 0)
        ring_round(0, 6)
        for unit in range(UNITS):
            wait_recv(pair_copy(unit))
        times = {1: (2, 2, 3), 2: (4, 5, 6), 3: (7, 8, 9), 4: (15, 18, 20), 5: (25, 28, 31)}
        for r, when in times.items():
            for m in range(3):
                at(when[m], ring_event, 1, r, m)
    else:
        order = tuple(range(UNITS))
        for e in range(n_exp):
            at(e, loads[e].wait)
        at(4, arrive, L_A, R_B)
        at(4, start, ring_gather(L_B))
        at(4, start, ring_gather(R_A))
        at(13, arrive, F_A, F_B)
        at(20, arrive, L_B, R_A)
        for k, unit in enumerate(order):
            at(n_exp * k, lambda unit=unit: wait_recv(pair_copy(unit)))

    steps = UNITS * n_exp
    tail = []
    for k, unit in enumerate(order):
        done = n_exp * (k + 1)
        at(done, lambda unit=unit: reduce_pair(unit).start())
        at(done + 2, add_pair, unit)
        if unit in (R_B, L_A, F_A, F_B):
            at(done + 3, lambda unit=unit: reduce_ring(unit).start())
    if first:
        at(27, add_far, R_A, F_A)
        at(28, lambda: reduce_ring(R_A).start())
        at(29, add_far, L_B, F_B)
        at(30, lambda: reduce_ring(L_B).start())
    else:
        at(steps + 6, add_far, R_A, F_A)
        at(steps + 6, lambda: reduce_ring(R_A).start())
        at(steps + 7, add_far, L_B, F_B)
        at(steps + 7, lambda: reduce_ring(L_B).start())

    def step_fn(step, carry):
        for t in sorted(plan):
            if t < steps:
                @pl.when(step == t)
                def _():
                    for action, args in plan[t]:
                        action(*args)

        k, e = step // n_exp, step % n_exp
        unit = k
        if first:
            unit = jnp.where(k < 2, k + F_A, jnp.where(k < 4, k, jnp.where(k < 6, k + 2, k - 6)))
        tokens = h_all[unit]
        gate_w = w_v[e, 0].reshape(-1, d_model)
        up_w = w_v[e, 1].reshape(-1, d_model)
        down_w = w_v[e, 2].reshape(-1, d_model)
        d_ff = gate_w.shape[0]
        inner = []
        for f in range(0, d_ff, 256):
            nt = (((1,), (1,)), ((), ()))
            u = lax.dot_general(tokens, gate_w[f:f + 256], nt, preferred_element_type=jnp.float32)
            v = lax.dot_general(tokens, up_w[f:f + 256], nt, preferred_element_type=jnp.float32)
            inner.append((jax.nn.silu(u) * v).astype(jnp.bfloat16))
        inner = jnp.concatenate(inner, axis=1)
        row = group * n_exp + e
        gate_cols = []
        for s in range(2):
            gates = g_all[unit, s, pl.ds(row, 1), :]
            gate_cols.append(jnp.broadcast_to(gates, (128, half)).T)
        gate_b = jnp.concatenate(gate_cols, axis=0)
        gate_b = jnp.concatenate([gate_b, gate_b], axis=1)
        start_sum = e == 0
        for c in range(0, d_model, 256):
            o = jnp.dot(inner, down_w[:, c:c + 256], preferred_element_type=jnp.float32)
            o = o.astype(jnp.bfloat16).astype(jnp.float32)
            part = jnp.where(gate_b >= 0.0, gate_b * o, 0.0)
            prev = jnp.where(start_sum, 0.0, acc[unit, :, c:c + 256])
            acc[unit, :, c:c + 256] = prev + part
        return carry

    lax.fori_loop(0, steps, step_fn, 0)

    for t in sorted(plan):
        if t >= steps:
            for action, args in plan[t]:
                action(*args)

    reduce_ring(R_B).wait_recv()
    reduce_ring(L_A).wait_recv()
    acc[O_B, 0:half, :] += x_ref[half:, :].astype(jnp.float32) + ring_in[0]
    acc[O_A, 0:half, :] += x_ref[:half, :].astype(jnp.float32) + ring_in[3]
    if first:
        ring_round(1, 6)
    reduce_ring(R_A).wait_recv()
    out_ref[0:half, :] = (acc[O_A, 0:half, :] + ring_in[2]).astype(out_ref.dtype)
    reduce_ring(L_B).wait_recv()
    out_ref[half:, :] = (acc[O_B, 0:half, :] + ring_in[5]).astype(out_ref.dtype)

    for unit in range(UNITS):
        wait_send(pair_copy(unit))
        reduce_pair(unit).wait_send()
        if unit in moves:
            wait_send(ring_gather(unit))
        if unit in sums:
            reduce_ring(unit).wait_send()
    if first:
        for layer in range(2):
            for m in range(3):
                for k in (1, 2, 3):
                    pre_copy(layer, m, k).wait_send()
                if with_ring:
                    for r in range(6):
                        for p in range(4):
                            ring_copy(layer, r, m, p).wait_send()


def moe_layer(first, ring_shape, hidden, gates, weights, stream):
    tok_dev, d_model = hidden.shape
    half = tok_dev // 2
    n_z, n_y, n_x = ring_shape
    vmem = pl.BlockSpec(memory_space=pltpu.VMEM)
    hbm = pl.BlockSpec(memory_space=pl.ANY)
    dma = pltpu.SemaphoreType.DMA
    if first:
        n_exp, f_dev = weights[0].shape[1] // n_x, weights[0].shape[2]
        w_shape = (n_exp, 3, n_z, n_y, n_x, f_dev, d_model)
    else:
        w_shape = weights[0].shape
        n_exp = w_shape[0]
    out_shape = [jax.ShapeDtypeStruct(stream.shape, stream.dtype)]
    out_specs = [vmem]
    extra = [dma((n_exp,))]
    if first:
        out_shape.append(jax.ShapeDtypeStruct(w_shape, jnp.bfloat16))
        out_specs.append(hbm)
        extra = [dma((6,)), dma((18,)), dma((18,)), dma((144,)), dma((144,))]
    return pl.pallas_call(
        functools.partial(layer_kernel, first, ring_shape),
        name="moe_first" if first else "moe_second",
        out_shape=out_shape,
        in_specs=[hbm, hbm] + [hbm] * len(weights) + [vmem],
        out_specs=out_specs,
        scratch_shapes=[
            pltpu.VMEM((UNITS, tok_dev, d_model), jnp.bfloat16),
            pltpu.VMEM((UNITS, 2, gates.shape[0], half), jnp.float32),
            pltpu.VMEM(w_shape, jnp.bfloat16),
            pltpu.VMEM((UNITS, tok_dev, d_model), jnp.float32),
            pltpu.VMEM((UNITS, half, d_model), jnp.float32),
            pltpu.VMEM((6, half, d_model), jnp.float32),
            dma((4,)),
            dma((12,)), dma((12,)), dma((16,)), dma((16,)), dma((8,)), dma((8,)), dma((6,)), dma((6,)),
        ] + extra,
        compiler_params=pltpu.CompilerParams(
            collective_id=0 if first else 1, has_side_effects=True, vmem_limit_bytes=67043328),
        cost_estimate=pl.CostEstimate(flops=52 * 10**9, bytes_accessed=16 * 2**20, transcendentals=0),
    )(hidden, gates, *weights, stream)


def solution(mesh):
    n_x = 4
    n_y = min(4, mesh.shape["fsdp"] // n_x)
    devices = mesh.devices.reshape(mesh.shape["rep"], mesh.shape["ep"], -1, n_y, n_x)
    cells = Mesh(devices, ("rep", "ep", "z", "y", "x"))
    ring_shape = devices.shape[2:]
    fsdp = ("z", "y", "x")
    token_spec = P(("rep", "ep") + fsdp, None)
    expert_in_spec = P(None, "ep", None, fsdp)
    expert_out_spec = P(None, "ep", fsdp, None)
    route_spec = P(None, ("rep", "ep") + fsdp, None)

    def device_step(x_in, norm_w, router_w, gate_w, up_w, down_w, routes):
        shards = (gate_w.transpose(0, 1, 3, 2), up_w.transpose(0, 1, 3, 2), down_w)
        hidden = rms_norm(x_in, norm_w[0])
        gates = dense_gates(hidden, router_w[0], routes[0])
        stream, weights = moe_layer(True, ring_shape, hidden, gates, shards, x_in)
        hidden = rms_norm(stream, norm_w[1])
        gates = dense_gates(hidden, router_w[1], routes[1])
        return moe_layer(False, ring_shape, hidden, gates, (weights,), stream)[0]

    return jax.shard_map(device_step, mesh=cells,
                         in_specs=(token_spec, P(), P(), expert_in_spec, expert_in_spec, expert_out_spec, route_spec),
                         out_specs=token_spec, check_vma=False)
```

time: 399 us -> 326 us (0.82)
  waiting for transfers between devices: 87.3 us -> 0 us
  Pallas kernels: 259 us -> 308 us
  blocking collectives: 24.5 us -> 0 us
  between operations: 13.6 us -> 0.08 us
    all_gather x2 -> x0, waiting for transfers between devices: 86.6 us -> none  [device_step(): lax.all_gather(swapped[l], ('z', 'y'), axis=0, tiled=True)]
    pallas_call x2, Pallas kernels: 259 us -> 308 us  [moe_layer(): pl.pallas_call(functools.partial(layer_kernel, first, ring_shape), name='...]
    all_to_all x1 -> x0, blocking collectives: 24.5 us -> none  [device_step(): swapped = lax.all_to_all(stacked, 'x', 1, 1, tiled=True)]
  transfers between devices with their start and end apart: 2 -> 0, of which waited for: 1 -> 0; matrix products, arithmetic and copies ran while one was open for 2% -> 0% of each run, Pallas kernels for 33% -> 0%
where the time goes in v2:
time: 326 us; the launch traced here: 324 us
  Pallas kernels  308 us (94%)
  other arithmetic  8.26 us (3%)
  local copies, waits for them, and re-layouts  6.32 us (2%)
    pallas_call x2, Pallas kernels, moe_layer(): pl.pallas_call(functools.partial(layer_kernel, first, ring_shape), name='...  308 us

profile of v2, /device:TPU:1, one launch (start us, length us, event | category | flops | bytes accessed | tf_op | source)
XLA Modules:
  0.0 323.6 jit_solution(4854987331941281)
XLA Ops:
  0.0 0.0 copy-start.3
  0.0 1.5 fusion
  1.6 1.4 fusion.22
  2.9 0.7 slice_bitcast_fusion
  3.7 0.7 fusion.6
  4.4 1.5 fusion.2.refs_0_
  5.9 0.0 copy-start
  5.9 1.0 copy-done
  6.9 0.0 copy-done.3
  6.9 0.4 select_reduce_fusion.3
  7.4 0.6 fusion.17.refs_1_
  8.0 186.4 %moe_first.1 = (bf16[512,1024]{1,0:T(8,128)(2,1)}, bf16[4,3,4,4,4,8,1024]{6,5,4,3,2,1,0:T(8,128)(2,1)}) custom-call(bf16[512,1024]{1,0:T(8,128)(2,1)} %copy-done, f32[32,512]{1,0:T(8,128)} %fusion.17.refs_1_, bf16[2,16,8,1024]{3,2,1,0:T(8,128)(2,1)} %bitcast.46, bf16[2,16,8,1024]{3,2,1,0:T(8,128)(2,1)} %bitcast.47, bf16[2,16,8,1024]{3,2,1,0:T(8,128)(2,1)} %refs_4_.1, ...), custom_call_target="tpu_custom_call" | custom-call | flops 51999997952 | bytes 16777216 | tf_op jit(solution)/shard_map/moe_first/pallas_call | solution.py:357
  194.4 0.0 copy-start.2
  194.4 0.0 copy-start.4
  194.4 1.5 fusion.3
  196.0 1.5 fusion.5.refs_0_
  197.5 0.0 copy-start.1
  197.5 1.0 copy-done.1
  198.5 0.0 copy-done.2
  198.5 0.0 copy-done.4
  198.5 0.4 select_reduce_fusion.1
  199.0 0.6 fusion.11.refs_1_
  199.6 121.7 %moe_second.1 = bf16[512,1024]{1,0:T(8,128)(2,1)} custom-call(bf16[512,1024]{1,0:T(8,128)(2,1)} %copy-done.1, f32[32,512]{1,0:T(8,128)} %fusion.11.refs_1_, bf16[4,3,4,4,4,8,1024]{6,5,4,3,2,1,0:T(8,128)(2,1)} %get-tuple-element.8.refs_2_, bf16[512,1024]{1,0:T(8,128)(2,1)} %get-tuple-element.7.refs_3_), custom_call_target="tpu_custom_call" | custom-call | flops 51999997952 | bytes 16777216 | tf_op jit(solution)/shard_map/moe_second/pallas_call | solution.py:357
  321.3 2.3 copy.11
  (4 shorter events, 0.1 us)
Async XLA Ops:
  0.0 6.9 %copy-start.3 = (bf16[2,1024,32]{1,2,0:T(8,128)(2,1)S(1)}, bf16[2,1024,32]{1,2,0:T(8,128)(2,1)}, u32[]{:S(2)}) copy-start(bf16[2,1024,32]{1,2,0:T(8,128)(2,1)} %param.9) | copy-start | bytes 393220
  5.9 1.0 copy-start
  194.4 4.1 %copy-start.2 = (pred[512,32]{0,1:T(8,128)(4,1)S(1)}, pred[512,32]{0,1:T(8,128)(4,1)}, u32[]{:S(2)}) copy-start(pred[512,32]{0,1:T(8,128)(4,1)} %get-tuple-element.18) | copy-start | bytes 49156
  194.4 4.1 %copy-start.4 = (bf16[2,1024,32]{1,2,0:T(8,128)(2,1)S(1)}, bf16[2,1024,32]{1,2,0:T(8,128)(2,1)}, u32[]{:S(2)}) copy-start(bf16[2,1024,32]{1,2,0:T(8,128)(2,1)} %param.9) | copy-start | bytes 393220
  197.5 1.0 copy-start.1

commit v3 on v2

v3 whole, which is shorter than its diff:
```python
import functools

import jax
import jax.numpy as jnp
from jax import lax
from jax.experimental import pallas as pl
from jax.experimental.pallas import tpu as pltpu
from jax.sharding import Mesh, PartitionSpec as P

NORM_EPS = 1e-5
MESH_ID = pl.DeviceIdType.MESH

OWN, NEAR, FAR, MORE = range(4)
UNITS = 8


def rms_norm(stream, norm_row):
    widened = stream.astype(jnp.float32)
    inv_rms = lax.rsqrt(jnp.mean(widened * widened, axis=-1, keepdims=True) + NORM_EPS)
    return (widened * inv_rms * norm_row).astype(jnp.bfloat16)


def dense_gates(hidden, router_l, routes_l):
    experts = router_l.shape[1]
    logits = jnp.dot(hidden, router_l, preferred_element_type=jnp.float32)
    ids = jnp.arange(experts, dtype=routes_l.dtype)
    chosen = jnp.any(routes_l[:, :, None] == ids[None, None, :], axis=1)
    top = jnp.max(jnp.where(chosen, logits, -jnp.inf), axis=-1, keepdims=True)
    weight = jnp.where(chosen, jnp.exp(jnp.where(chosen, logits - top, 0.0)), 0.0)
    gates = weight / jnp.sum(weight, axis=-1, keepdims=True)
    return jnp.where(chosen, gates, -1.0).T


def layer_kernel(first, ring_shape, *refs):
    if first:
        (h_ref, g_ref, gate_ref, up_ref, down_ref, x_ref, out_ref, next_ref, h_all, g_all, w_v, acc, pair_in, ring_in,
         own_sem, ag_send, ag_recv, agp_send, agp_recv, pair_send, pair_recv, ring_send, ring_recv,
         pre_own, pre_send, pre_recv, wr_send, wr_recv) = refs
    else:
        (h_ref, g_ref, w_ref, x_ref, out_ref, h_all, g_all, w_v, acc, pair_in, ring_in,
         own_sem, ag_send, ag_recv, agp_send, agp_recv, pair_send, pair_recv, ring_send, ring_recv, w_sem) = refs
    part, d_model = h_all.shape[3], h_all.shape[4]
    n_exp = w_v.shape[0]
    n_z, n_y, n_x = ring_shape
    ep, x = lax.axis_index("ep"), lax.axis_index("x")
    z, y = lax.axis_index("z"), lax.axis_index("y")
    partner = {"ep": 1 - ep}
    owner = lax.rem(x + y, 4)
    group = ep * 4 + owner

    def remote(src, dst, send, recv, peer):
        return pltpu.make_async_remote_copy(src, dst, send, recv, device_id=peer, device_id_type=MESH_ID)

    def beside(axis, stream):
        move = 1 + 2 * stream
        return {"x": lax.rem(x + (1 - axis) * move, 4), "y": lax.rem(y + axis * move, 4)}

    def diagonal(step):
        return {"x": lax.rem(x + 4 - step, 4), "y": lax.rem(y + 4 + step, 4)}

    peers = [beside(axis, stream) for axis in range(2) for stream in range(2)] + [partner]
    if first:
        peers.append({"x": lax.rem(x + 2, 4)})
        peers += [diagonal(1), diagonal(-1)]
        if n_z > 1:
            peers += [{"z": lax.rem(z + 1, n_z)}, {"z": lax.rem(z + n_z - 1, n_z)}]
    barrier = pltpu.get_barrier_semaphore()
    for peer in peers:
        pl.semaphore_signal(barrier, inc=1, device_id=peer, device_id_type=MESH_ID)

    own = []
    for axis in range(2):
        for t in range(2):
            idx = 2 * axis + t
            rows = pl.ds(idx * part, part)
            own.append(pltpu.make_async_copy(h_ref.at[rows], h_all.at[axis, t, 0], own_sem.at[2 * idx]))
            own.append(pltpu.make_async_copy(g_ref.at[:, rows], g_all.at[axis, t, 0], own_sem.at[2 * idx + 1]))

    if first:
        sources = (gate_ref, up_ref, down_ref)
        targets = (w_v, next_ref)

        def pre_local(layer, m):
            return pltpu.make_async_copy(
                sources[m].at[layer, pl.ds(owner * n_exp, n_exp)], targets[layer].at[:, m, z, y, x],
                pre_own.at[layer * 3 + m])

        def pre_copy(layer, m, k):
            idx = (layer * 3 + m) * 3 + k - 1
            return remote(sources[m].at[layer, pl.ds(lax.rem(owner + k, 4) * n_exp, n_exp)],
                          targets[layer].at[:, m, z, y, x],
                          pre_send.at[idx], pre_recv.at[idx], {"x": lax.rem(x + k, 4)})

        def z_first(m, p):
            return m == p // 2

        def rounds(m, p):
            sizes = (n_z, n_y) if z_first(m, p) else (n_y, n_z)
            return [r for r in range(6) if sizes[r // 3] > 1]

        def ring_copy(layer, r, m, p):
            buf = targets[layer]
            step = 1 if p % 2 == 0 else -1
            along_z = (r < 3) == z_first(m, p)
            pos = z if along_z else y
            i = lax.rem(pos + 4 - step * (r % 3), 4)
            if r < 3:
                piece = buf.at[p, m, i, y] if along_z else buf.at[p, m, z, i]
            else:
                piece = buf.at[p, m, i] if along_z else buf.at[p, m, :, i]
            idx = ((layer * 6 + r) * 3 + m) * 4 + p
            peer = {"z": lax.rem(z + 4 + step, 4)} if along_z else diagonal(step)
            return remote(piece, piece, wr_send.at[idx], wr_recv.at[idx], peer)

        def pre_start(layer):
            for m in range(3):
                for k in (1, 3, 2):
                    pre_copy(layer, m, k).start()
                pre_local(layer, m).start()

        def pre_wait(layer, m):
            pre_local(layer, m).wait()
            for k in (1, 3, 2):
                pre_copy(layer, m, k).wait_recv()

        def ring_event(layer, r, m):
            with jax.named_scope(f"w{layer}r{r}m{m}"):
                if r == 0:
                    pre_wait(layer, m)
                for p in range(4):
                    before = [q for q in rounds(m, p) if q < r]
                    if r in rounds(m, p) or r == 6:
                        if before:
                            ring_copy(layer, before[-1], m, p).wait_recv()
                    if r in rounds(m, p):
                        ring_copy(layer, r, m, p).start()

        def ring_round(layer, r):
            for m in range(3):
                ring_event(layer, r, m)
    else:
        loads = [pltpu.make_async_copy(w_ref.at[e], w_v.at[e], w_sem.at[e]) for e in range(n_exp)]

    def pair_copy(unit):
        return (
            remote(h_all.at[unit, :, 0], h_all.at[unit, :, 1], agp_send.at[unit], agp_recv.at[unit], partner),
            remote(g_all.at[unit, :, 0], g_all.at[unit, :, 1], agp_send.at[8 + unit], agp_recv.at[8 + unit], partner),
        )

    def gather(axis, kind, t):
        src_kind, src_t, to = {
            (NEAR, 1): (OWN, 0, 0), (MORE, 1): (OWN, 1, 0), (FAR, 0): (NEAR, 1, 0),
            (NEAR, 0): (OWN, 1, 1), (MORE, 0): (OWN, 0, 1), (FAR, 1): (NEAR, 0, 1),
        }[kind, t]
        src, dst = 2 * src_kind + axis, 2 * kind + axis
        idx = 2 * (dst - 2) + t
        peer = beside(axis, to)
        return (
            remote(h_all.at[src, src_t, 0], h_all.at[dst, t, 0], ag_send.at[idx], ag_recv.at[idx], peer),
            remote(g_all.at[src, src_t, 0], g_all.at[dst, t, 0], ag_send.at[12 + idx], ag_recv.at[12 + idx], peer),
        )

    def start(copies):
        for copy in copies:
            copy.start()

    def wait_recv(copies):
        for copy in copies:
            copy.wait_recv()

    def wait_send(copies):
        for copy in copies:
            copy.wait_send()

    def gather_start(kind):
        for axis in range(2):
            for t in range(2):
                start(gather(axis, kind, t))

    def arrive(kind):
        with jax.named_scope(f"arr{kind}"):
            for axis in range(2):
                for t in range(2):
                    wait_recv(gather(axis, kind, t))
                    if kind == NEAR:
                        start(gather(axis, FAR, 1 - t))
                start(pair_copy(2 * kind + axis))

    def reduce_pair(unit):
        return remote(acc.at[unit, :, 1], pair_in.at[unit], pair_send.at[unit], pair_recv.at[unit], partner)

    def reduce_ring(unit, t):
        slot = 2 * (unit - 2) + t
        return remote(acc.at[unit, t, 0], ring_in.at[slot], ring_send.at[slot], ring_recv.at[slot],
                      beside(unit % 2, t))

    def add_pair(unit):
        with jax.named_scope("pairw"):
            reduce_pair(unit).wait_recv()
        acc[unit, :, 0] += pair_in[unit]

    def add_more(unit):
        with jax.named_scope("morew"):
            reduce_pair(unit).wait_recv()
            far = unit - 2 * (MORE - FAR)
            for t in range(2):
                reduce_ring(far, t).wait_recv()
        for t in range(2):
            acc[unit, t, 0] += pair_in[unit, t] + ring_in[2 * (far - 2) + t]

    def ring_start(unit):
        for t in range(2):
            reduce_ring(unit, t).start()

    for copy in own:
        copy.start()
    if not first:
        start(loads)
    for copy in own:
        copy.wait()
    with jax.named_scope("barrier"):
        pl.semaphore_wait(barrier, len(peers))
    if first:
        pre_start(0)
    gather_start(NEAR)
    for axis in range(2):
        start(pair_copy(axis))
    gather_start(MORE)

    steps = UNITS * n_exp
    plan = {}

    def at(t, action, *args):
        plan.setdefault(t, []).append((action, args))

    if first:
        kinds = (FAR, NEAR, MORE, OWN)
        for r in range(3):
            ring_round(0, r)
        arrive(NEAR)
        pre_start(1)
        ring_round(0, 3)
        arrive(MORE)
        ring_round(0, 4)
        arrive(FAR)
        ring_round(0, 5)
        ring_round(1, 0)
        ring_round(0, 6)
        for unit in range(UNITS):
            wait_recv(pair_copy(unit))
        times = {1: (2, 2, 3), 2: (5, 5, 6), 3: (8, 8, 9), 4: (16, 18, 20), 5: (28, 30, 31)}
        for r, when in times.items():
            for m in range(3):
                at(when[m], ring_event, 1, r, m)
    else:
        kinds = (OWN, NEAR, FAR, MORE)
        for e in range(n_exp):
            at(e, loads[e].wait)
        at(3, arrive, NEAR)
        at(6, arrive, MORE)
        at(9, arrive, FAR)

    def unit_of(k):
        turn, axis = k // 2, k % 2
        kind = turn
        if first:
            kind = jnp.where(turn == 0, FAR, jnp.where(turn == 1, NEAR, jnp.where(turn == 2, MORE, OWN)))
        return 2 * kind + axis

    more_turn, own_turn = kinds.index(MORE), kinds.index(OWN)

    def finished(k, e):
        before = unit_of(k - 1)
        turn = (k - 1) // 2

        @pl.when(e == 0)
        def _():
            reduce_pair(before).start()

        @pl.when((e == 2) & (turn != more_turn))
        def _():
            add_pair(before)

        @pl.when((e == 3) & (turn != own_turn) & (turn != more_turn))
        def _():
            ring_start(before)

        if first:
            late = unit_of(k - 2)

            @pl.when((e == 2) & ((k - 2) // 2 == more_turn) & (k >= 2))
            def _():
                add_more(late)

            @pl.when((e == 3) & ((k - 2) // 2 == more_turn) & (k >= 2))
            def _():
                ring_start(late)

    def step_fn(step, carry):
        k, e = step // n_exp, step % n_exp
        for t in sorted(plan):
            @pl.when(step == t)
            def _():
                for action, args in plan[t]:
                    action(*args)

        @pl.when(k >= 1)
        def _():
            finished(k, e)

        unit = unit_of(k)
        if not first:
            @pl.when(e == 0)
            def _():
                wait_recv(pair_copy(unit))

        with jax.named_scope("load"):
            tokens = h_all[unit].reshape(-1, d_model)
        gate_w = w_v[e, 0].reshape(-1, d_model)
        up_w = w_v[e, 1].reshape(-1, d_model)
        down_w = w_v[e, 2].reshape(-1, d_model)
        d_ff = gate_w.shape[0]
        inner = []
        for f in range(0, d_ff, 256):
            nt = (((1,), (1,)), ((), ()))
            u = lax.dot_general(tokens, gate_w[f:f + 256], nt, preferred_element_type=jnp.float32)
            v = lax.dot_general(tokens, up_w[f:f + 256], nt, preferred_element_type=jnp.float32)
            inner.append((jax.nn.silu(u) * v).astype(jnp.bfloat16))
        inner = jnp.concatenate(inner, axis=1)
        row = group * n_exp + e
        gate_cols = []
        for t in range(2):
            for s in range(2):
                gates = g_all[unit, t, s, pl.ds(row, 1), :]
                gate_cols.append(jnp.broadcast_to(gates, (128, part)).T)
        gate_b = jnp.concatenate(gate_cols, axis=0)
        gate_b = jnp.concatenate([gate_b, gate_b], axis=1)
        start_sum = e == 0
        for c in range(0, d_model, 256):
            o = jnp.dot(inner, down_w[:, c:c + 256], preferred_element_type=jnp.float32)
            o = o.astype(jnp.bfloat16).astype(jnp.float32)
            new = jnp.where(gate_b >= 0.0, gate_b * o, 0.0).reshape(2, 2, part, 256)
            prev = jnp.where(start_sum, 0.0, acc[unit, :, :, :, c:c + 256])
            acc[unit, :, :, :, c:c + 256] = prev + new
        return carry

    lax.fori_loop(0, steps, step_fn, 0)

    last = 2 * kinds[3] + 1
    reduce_pair(last).start()
    if first:
        add_pair(last)
    else:
        add_more(last - 1)
        ring_start(last - 1)
        add_more(last)
        ring_start(last)

    for axis in range(2):
        near, more = 2 * NEAR + axis, 2 * MORE + axis
        for t in range(2):
            with jax.named_scope("fin1"):
                reduce_ring(near, 1 - t).wait_recv()
            rows = pl.ds((2 * axis + t) * part, part)
            acc[axis, t, 0] += x_ref[rows, :].astype(jnp.float32) + ring_in[2 * (near - 2) + 1 - t]
    if first:
        ring_round(1, 6)
    for axis in range(2):
        more = 2 * MORE + axis
        for t in range(2):
            with jax.named_scope("fin2"):
                reduce_ring(more, t).wait_recv()
            rows = pl.ds((2 * axis + t) * part, part)
            out_ref[rows, :] = (acc[axis, t, 0] + ring_in[2 * (more - 2) + t]).astype(out_ref.dtype)

    for unit in range(UNITS):
        wait_send(pair_copy(unit))
        reduce_pair(unit).wait_send()
        if unit >= 2:
            for t in range(2):
                wait_send(gather(unit % 2, unit // 2, t))
                reduce_ring(unit, t).wait_send()
    if first:
        for layer in range(2):
            for m in range(3):
                for k in (1, 2, 3):
                    pre_copy(layer, m, k).wait_send()
                for p in range(4):
                    for r in rounds(m, p):
                        ring_copy(layer, r, m, p).wait_send()


def moe_layer(first, ring_shape, hidden, gates, weights, stream):
    tok_dev, d_model = hidden.shape
    part = tok_dev // 4
    n_z, n_y, n_x = ring_shape
    vmem = pl.BlockSpec(memory_space=pltpu.VMEM)
    hbm = pl.BlockSpec(memory_space=pl.ANY)
    dma = pltpu.SemaphoreType.DMA
    if first:
        n_exp, f_dev = weights[0].shape[1] // n_x, weights[0].shape[2]
        w_shape = (n_exp, 3, n_z, n_y, n_x, f_dev, d_model)
    else:
        w_shape = weights[0].shape
        n_exp = w_shape[0]
    out_shape = [jax.ShapeDtypeStruct(stream.shape, stream.dtype)]
    out_specs = [vmem]
    extra = [dma((n_exp,))]
    if first:
        out_shape.append(jax.ShapeDtypeStruct(w_shape, jnp.bfloat16))
        out_specs.append(hbm)
        extra = [dma((6,)), dma((18,)), dma((18,)), dma((144,)), dma((144,))]
    return pl.pallas_call(
        functools.partial(layer_kernel, first, ring_shape),
        name="moe_first" if first else "moe_second",
        out_shape=out_shape,
        in_specs=[hbm, hbm] + [hbm] * len(weights) + [vmem],
        out_specs=out_specs,
        scratch_shapes=[
            pltpu.VMEM((UNITS, 2, 2, part, d_model), jnp.bfloat16),
            pltpu.VMEM((UNITS, 2, 2, gates.shape[0], part), jnp.float32),
            pltpu.VMEM(w_shape, jnp.bfloat16),
            pltpu.VMEM((UNITS, 2, 2, part, d_model), jnp.float32),
            pltpu.VMEM((UNITS, 2, part, d_model), jnp.float32),
            pltpu.VMEM((12, part, d_model), jnp.float32),
            dma((8,)),
            dma((24,)), dma((24,)), dma((16,)), dma((16,)), dma((8,)), dma((8,)), dma((12,)), dma((12,)),
        ] + extra,
        compiler_params=pltpu.CompilerParams(
            collective_id=0 if first else 1, has_side_effects=True, vmem_limit_bytes=67043328),
        cost_estimate=pl.CostEstimate(flops=52 * 10**9, bytes_accessed=16 * 2**20, transcendentals=0),
    )(hidden, gates, *weights, stream)


def solution(mesh):
    n_x = 4
    n_y = min(4, mesh.shape["fsdp"] // n_x)
    devices = mesh.devices.reshape(mesh.shape["rep"], mesh.shape["ep"], -1, n_y, n_x)
    cells = Mesh(devices, ("rep", "ep", "z", "y", "x"))
    ring_shape = devices.shape[2:]
    fsdp = ("z", "y", "x")
    token_spec = P(("rep", "ep") + fsdp, None)
    expert_in_spec = P(None, "ep", None, fsdp)
    expert_out_spec = P(None, "ep", fsdp, None)
    route_spec = P(None, ("rep", "ep") + fsdp, None)

    def device_step(x_in, norm_w, router_w, gate_w, up_w, down_w, routes):
        shards = (gate_w.transpose(0, 1, 3, 2), up_w.transpose(0, 1, 3, 2), down_w)
        hidden = rms_norm(x_in, norm_w[0])
        gates = dense_gates(hidden, router_w[0], routes[0])
        stream, weights = moe_layer(True, ring_shape, hidden, gates, shards, x_in)
        hidden = rms_norm(stream, norm_w[1])
        gates = dense_gates(hidden, router_w[1], routes[1])
        return moe_layer(False, ring_shape, hidden, gates, (weights,), stream)[0]

    return jax.shard_map(device_step, mesh=cells,
                         in_specs=(token_spec, P(), P(), expert_in_spec, expert_in_spec, expert_out_spec, route_spec),
                         out_specs=token_spec, check_vma=False)
```

time: 326 us -> 328 us (level)
  Pallas kernels: 308 us -> 312 us
    pallas_call x2, Pallas kernels: 308 us -> 312 us  [moe_layer(): pl.pallas_call(functools.partial(layer_kernel, first, ring_shape), name='...]
where the time goes in v3:
time: 328 us; the launch traced here: 327 us
  Pallas kernels  312 us (95%)
  other arithmetic  8.26 us (3%)
  local copies, waits for them, and re-layouts  6.32 us (2%)
    pallas_call x2, Pallas kernels, moe_layer(): pl.pallas_call(functools.partial(layer_kernel, first, ring_shape), name='...  312 us

profile of v3, /device:TPU:1, one launch (start us, length us, event | category | flops | bytes accessed | tf_op | source)
XLA Modules:
  0.0 327.2 jit_solution(1969285889685652667)
XLA Ops:
  0.0 0.0 copy-start.3
  0.0 1.5 fusion
  1.6 1.4 fusion.22
  2.9 0.7 slice_bitcast_fusion
  3.7 0.7 fusion.6
  4.4 1.5 fusion.2.refs_0_
  5.9 0.0 copy-start
  5.9 1.0 copy-done
  6.9 0.0 copy-done.3
  6.9 0.4 select_reduce_fusion.3
  7.4 0.6 fusion.17.refs_1_
  8.0 218.8 %moe_first.1 = (bf16[512,1024]{1,0:T(8,128)(2,1)}, bf16[4,3,4,4,4,8,1024]{6,5,4,3,2,1,0:T(8,128)(2,1)}) custom-call(bf16[512,1024]{1,0:T(8,128)(2,1)} %copy-done, f32[32,512]{1,0:T(8,128)} %fusion.17.refs_1_, bf16[2,16,8,1024]{3,2,1,0:T(8,128)(2,1)} %bitcast.46, bf16[2,16,8,1024]{3,2,1,0:T(8,128)(2,1)} %bitcast.47, bf16[2,16,8,1024]{3,2,1,0:T(8,128)(2,1)} %refs_4_.1, ...), custom_call_target="tpu_custom_call" | custom-call | flops 51999997952 | bytes 16777216 | tf_op jit(solution)/shard_map/moe_first/pallas_call | solution.py:413
  226.8 0.0 copy-start.2
  226.8 0.0 copy-start.4
  226.8 1.5 fusion.3
  228.4 1.5 fusion.5.refs_0_
  229.9 0.0 copy-start.1
  230.0 1.0 copy-done.1
  230.9 0.0 copy-done.2
  230.9 0.0 copy-done.4
  230.9 0.4 select_reduce_fusion.1
  231.4 0.6 fusion.11.refs_1_
  232.0 92.9 %moe_second.1 = bf16[512,1024]{1,0:T(8,128)(2,1)} custom-call(bf16[512,1024]{1,0:T(8,128)(2,1)} %copy-done.1, f32[32,512]{1,0:T(8,128)} %fusion.11.refs_1_, bf16[4,3,4,4,4,8,1024]{6,5,4,3,2,1,0:T(8,128)(2,1)} %get-tuple-element.8.refs_2_, bf16[512,1024]{1,0:T(8,128)(2,1)} %get-tuple-element.7.refs_3_), custom_call_target="tpu_custom_call" | custom-call | flops 51999997952 | bytes 16777216 | tf_op jit(solution)/shard_map/moe_second/pallas_call | solution.py:413
  325.0 2.3 copy.11
  (4 shorter events, 0.1 us)
Async XLA Ops:
  0.0 6.9 %copy-start.3 = (bf16[2,1024,32]{1,2,0:T(8,128)(2,1)S(1)}, bf16[2,1024,32]{1,2,0:T(8,128)(2,1)}, u32[]{:S(2)}) copy-start(bf16[2,1024,32]{1,2,0:T(8,128)(2,1)} %param.9) | copy-start | bytes 393220
  5.9 1.0 copy-start
  226.8 4.1 %copy-start.2 = (pred[512,32]{0,1:T(8,128)(4,1)S(1)}, pred[512,32]{0,1:T(8,128)(4,1)}, u32[]{:S(2)}) copy-start(pred[512,32]{0,1:T(8,128)(4,1)} %get-tuple-element.18) | copy-start | bytes 49156
  226.8 4.1 %copy-start.4 = (bf16[2,1024,32]{1,2,0:T(8,128)(2,1)S(1)}, bf16[2,1024,32]{1,2,0:T(8,128)(2,1)}, u32[]{:S(2)}) copy-start(bf16[2,1024,32]{1,2,0:T(8,128)(2,1)} %param.9) | copy-start | bytes 393220
  229.9 1.0 copy-start.1

commit v4 on v0

v4 whole, which is shorter than its diff:
```python
import functools

import jax
import jax.numpy as jnp
from jax import lax
from jax.experimental import pallas as pl
from jax.experimental.pallas import tpu as pltpu
from jax.sharding import Mesh, PartitionSpec as P

NORM_EPS = 1e-5
MESH_ID = pl.DeviceIdType.MESH

OWN, NEAR, FAR, MORE = range(4)
UNITS = 8
TWO_RINGS = True
W1_TIMES = {4: (13, 17, 21), 5: (25, 29, 31)}


def kernel(ring_shape, x_ref, norm_ref, router_ref, routes_ref, gate_ref, up_ref, down_ref, out_ref, next_ref,
           h_all, g_all, w_v, acc, pair_in, ring_in,
           ag_send, ag_recv, agp_send, agp_recv, pair_send, pair_recv, ring_send, ring_recv,
           pre_own, pre_send, pre_recv, wr_send, wr_recv, w_sem, ready):
    part, d_model = h_all.shape[3], h_all.shape[4]
    n_exp = w_v.shape[0]
    n_z, n_y, n_x = ring_shape
    ep, x = lax.axis_index("ep"), lax.axis_index("x")
    z, y = lax.axis_index("z"), lax.axis_index("y")
    partner = {"ep": 1 - ep}
    owners = (x, lax.rem(x + y, 4) if TWO_RINGS else x)
    steps = UNITS * n_exp

    def remote(src, dst, send, recv, peer):
        return pltpu.make_async_remote_copy(src, dst, send, recv, device_id=peer, device_id_type=MESH_ID)

    def beside(layer, axis, stream):
        move = 1 + 2 * stream
        if layer == 0 or not TWO_RINGS:
            return {"x": lax.rem(x + move, 4)}
        return {"x": lax.rem(x + (1 - axis) * move, 4), "y": lax.rem(y + axis * move, 4)}

    def next_row(layer, step):
        if layer == 0 or not TWO_RINGS:
            return {"y": lax.rem(y + 4 + step, 4)}
        return {"x": lax.rem(x + 4 - step, 4), "y": lax.rem(y + 4 + step, 4)}

    token_peers = [beside(0, 0, 0), beside(0, 0, 1), partner]
    if TWO_RINGS:
        token_peers += [beside(1, 1, 0), beside(1, 1, 1)]
    peers = token_peers + [{"x": lax.rem(x + 2, 4)}] + [next_row(1, step) for step in (1, -1)]
    if n_z > 1:
        peers += [{"z": lax.rem(z + 1, n_z)}, {"z": lax.rem(z + n_z - 1, n_z)}]
    barrier = pltpu.get_barrier_semaphore()
    for peer in peers:
        pl.semaphore_signal(barrier, inc=1, device_id=peer, device_id_type=MESH_ID)

    sources = (gate_ref, up_ref, down_ref)
    targets = (w_v, next_ref)

    def pre_local(layer, m):
        return pltpu.make_async_copy(
            sources[m].at[layer, pl.ds(owners[layer] * n_exp, n_exp)], targets[layer].at[:, m, z, y, x],
            pre_own.at[layer * 3 + m])

    def pre_copy(layer, m, k):
        idx = (layer * 3 + m) * 3 + k - 1
        return remote(sources[m].at[layer, pl.ds(lax.rem(owners[layer] + k, 4) * n_exp, n_exp)],
                      targets[layer].at[:, m, z, y, x],
                      pre_send.at[idx], pre_recv.at[idx], {"x": lax.rem(x + k, 4)})

    def z_first(layer, m, p):
        return p < 2 and (layer == 0 or not TWO_RINGS or m == 1)

    def rounds(layer, m, p):
        sizes = (n_z, n_y) if z_first(layer, m, p) else (n_y, n_z)
        return [r for r in range(6) if sizes[r // 3] > 1]

    def ring_copy(layer, r, m, p):
        buf = targets[layer]
        step = 1 if p % 2 == 0 else -1
        along_z = (r < 3) == z_first(layer, m, p)
        pos = z if along_z else y
        i = lax.rem(pos + 4 - step * (r % 3), 4)
        if r < 3:
            piece = buf.at[p, m, i, y] if along_z else buf.at[p, m, z, i]
        else:
            piece = buf.at[p, m, i] if along_z else buf.at[p, m, :, i]
        idx = ((layer * 6 + r) * 3 + m) * 4 + p
        peer = {"z": lax.rem(z + 4 + step, 4)} if along_z else next_row(layer, step)
        return remote(piece, piece, wr_send.at[idx], wr_recv.at[idx], peer)

    def pre_start(layer):
        for m in range(3):
            for k in (1, 3, 2):
                pre_copy(layer, m, k).start()
            pre_local(layer, m).start()

    def ring_event(layer, r, m):
        with jax.named_scope(f"w{layer}r{r}m{m}"):
            if r == 0:
                pre_local(layer, m).wait()
                for k in (1, 3, 2):
                    pre_copy(layer, m, k).wait_recv()
            for p in range(4):
                before = [q for q in rounds(layer, m, p) if q < r]
                if (r in rounds(layer, m, p) or r == 6) and before:
                    ring_copy(layer, before[-1], m, p).wait_recv()
                if r in rounds(layer, m, p):
                    ring_copy(layer, r, m, p).start()

    def ring_round(layer, r):
        for m in range(3):
            ring_event(layer, r, m)

    loads = [pltpu.make_async_copy(next_ref.at[e], w_v.at[e], w_sem.at[e]) for e in range(n_exp)]

    def prepare(layer, stream_ref):
        experts = router_ref.shape[1]
        for axis in range(2):
            for t in range(2):
                rows = pl.ds((2 * axis + t) * part, part)
                wide = stream_ref[rows, :].astype(jnp.float32)
                inv_rms = lax.rsqrt(jnp.mean(wide * wide, axis=-1, keepdims=True) + NORM_EPS)
                hidden = (wide * inv_rms * norm_ref[layer:layer + 1, :]).astype(jnp.bfloat16)
                h_all[axis, t, 0] = hidden
                logits = lax.dot_general(router_ref[layer], hidden, (((1,), (1,)), ((), ())),
                                         preferred_element_type=jnp.float32)
                ids = lax.broadcasted_iota(jnp.int32, (experts, part), 0)
                chosen = ids < 0
                for j in range(routes_ref.shape[1]):
                    chosen |= routes_ref[layer, j:j + 1, (2 * axis + t) * part:(2 * axis + t + 1) * part] == ids
                top = jnp.max(jnp.where(chosen, logits, -jnp.inf), axis=0, keepdims=True)
                weight = jnp.where(chosen, jnp.exp(jnp.where(chosen, logits - top, 0.0)), 0.0)
                gates = weight / jnp.sum(weight, axis=0, keepdims=True)
                g_all[axis, t, 0] = jnp.where(chosen, gates, -1.0)

    def start(copies):
        for copy in copies:
            copy.start()

    def wait_recv(copies):
        for copy in copies:
            copy.wait_recv()

    def wait_send(copies):
        for copy in copies:
            copy.wait_send()

    def run_layer(layer, stream_ref):
        first = layer == 0
        group = ep * 4 + owners[layer]

        def pair_copy(unit):
            return (
                remote(h_all.at[unit, :, 0], h_all.at[unit, :, 1],
                       agp_send.at[layer, unit], agp_recv.at[layer, unit], partner),
                remote(g_all.at[unit, :, 0], g_all.at[unit, :, 1],
                       agp_send.at[layer, 8 + unit], agp_recv.at[layer, 8 + unit], partner),
            )

        def gather(axis, kind, t):
            src_kind, src_t, to = {
                (NEAR, 1): (OWN, 0, 0), (MORE, 1): (OWN, 1, 0), (FAR, 0): (NEAR, 1, 0),
                (NEAR, 0): (OWN, 1, 1), (MORE, 0): (OWN, 0, 1), (FAR, 1): (NEAR, 0, 1),
            }[kind, t]
            src, dst = 2 * src_kind + axis, 2 * kind + axis
            idx = 2 * (dst - 2) + t
            peer = beside(layer, axis, to)
            return (
                remote(h_all.at[src, src_t, 0], h_all.at[dst, t, 0],
                       ag_send.at[layer, idx], ag_recv.at[layer, idx], peer),
                remote(g_all.at[src, src_t, 0], g_all.at[dst, t, 0],
                       ag_send.at[layer, 12 + idx], ag_recv.at[layer, 12 + idx], peer),
            )

        def gather_start(kind):
            for axis in range(2):
                for t in range(2):
                    start(gather(axis, kind, t))

        def arrive(kind):
            with jax.named_scope(f"arr{kind}"):
                for axis in range(2):
                    for t in range(2):
                        wait_recv(gather(axis, kind, t))
                        if kind == NEAR:
                            start(gather(axis, FAR, 1 - t))
                    start(pair_copy(2 * kind + axis))

        def reduce_pair(unit):
            return remote(acc.at[unit, :, 1], pair_in.at[unit],
                          pair_send.at[layer, unit], pair_recv.at[layer, unit], partner)

        def reduce_ring(unit, t):
            slot = 2 * (unit - 2) + t
            return remote(acc.at[unit, t, 0], ring_in.at[slot], ring_send.at[layer, slot], ring_recv.at[layer, slot],
                          beside(layer, unit % 2, t))

        def add_pair(unit):
            with jax.named_scope("pairw"):
                reduce_pair(unit).wait_recv()
            acc[unit, :, 0] += pair_in[unit]

        def add_more(unit):
            with jax.named_scope("morew"):
                reduce_pair(unit).wait_recv()
                far = unit - 2 * (MORE - FAR)
                for t in range(2):
                    reduce_ring(far, t).wait_recv()
            for t in range(2):
                acc[unit, t, 0] += pair_in[unit, t] + ring_in[2 * (far - 2) + t]

        def ring_start(unit):
            for t in range(2):
                reduce_ring(unit, t).start()

        plan = {}

        def at(t, action, *args):
            plan.setdefault(t, []).append((action, args))

        prepare(layer, stream_ref)
        if not first:
            with jax.named_scope("ready"):
                pl.semaphore_wait(ready, len(token_peers))
        gather_start(NEAR)
        for axis in range(2):
            start(pair_copy(axis))
        gather_start(MORE)
        if first:
            for r in range(3):
                ring_round(0, r)
            arrive(NEAR)
            pre_start(1)
            ring_round(0, 3)
            ring_round(0, 4)
            arrive(MORE)
            ring_round(0, 5)
            arrive(FAR)
            ring_round(1, 0)
            ring_round(0, 6)
            for unit in range(UNITS):
                wait_recv(pair_copy(unit))
            for t, r in ((1, 1), (3, 2), (5, 3)):
                at(t, ring_round, 1, r)
            for r, when in W1_TIMES.items():
                for m in range(3):
                    at(when[m], ring_event, 1, r, m)
        else:
            ring_round(1, 6)
            start(loads)
            for e in range(n_exp):
                at(e, loads[e].wait)
            at(3, arrive, NEAR)
            at(6, arrive, MORE)
            at(9, arrive, FAR)

        def unit_of(k):
            if first:
                return jnp.where(k < 2, k + 2 * FAR, jnp.where(k < 4, k, jnp.where(k < 6, k + 2, k - 6)))
            return jnp.where(k == 0, 0, jnp.where(k == UNITS - 1, 1, k + 1))

        def step_fn(step, carry):
            k, e = step // n_exp, step % n_exp
            before, late = unit_of(k - 1), unit_of(k - 2)
            kind, late_kind = before // 2, late // 2

            def planned(e_static):
                for t in sorted(plan):
                    if t % n_exp == e_static:
                        @pl.when(k == t // n_exp)
                        def _():
                            for action, args in plan[t]:
                                action(*args)

            @pl.when(e == 0)
            def _():
                planned(0)

                @pl.when(k >= 1)
                def _():
                    reduce_pair(before).start()

                if not first:
                    wait_recv(pair_copy(unit_of(k)))

            @pl.when(e == 1)
            def _():
                planned(1)

            @pl.when(e == 2)
            def _():
                planned(2)

                @pl.when((k >= 1) & (kind != MORE))
                def _():
                    add_pair(before)

                @pl.when((k >= 2) & (late_kind == MORE) if first else (k >= 1) & (kind == MORE))
                def _():
                    add_more(late if first else before)

            @pl.when(e == 3)
            def _():
                planned(3)

                @pl.when((k >= 1) & (kind != OWN) & ((kind != MORE) if first else True))
                def _():
                    ring_start(before)

                if first:
                    @pl.when((k >= 2) & (late_kind == MORE))
                    def _():
                        ring_start(late)

            unit = unit_of(k)
            with jax.named_scope("load"):
                tokens = h_all[unit].reshape(-1, d_model)
            gate_w = w_v[e, 0].reshape(-1, d_model)
            up_w = w_v[e, 1].reshape(-1, d_model)
            down_w = w_v[e, 2].reshape(-1, d_model)
            d_ff = gate_w.shape[0]
            inner = []
            for f in range(0, d_ff, 256):
                nt = (((1,), (1,)), ((), ()))
                u = lax.dot_general(tokens, gate_w[f:f + 256], nt, preferred_element_type=jnp.float32)
                v = lax.dot_general(tokens, up_w[f:f + 256], nt, preferred_element_type=jnp.float32)
                inner.append((jax.nn.silu(u) * v).astype(jnp.bfloat16))
            inner = jnp.concatenate(inner, axis=1)
            row = group * n_exp + e
            gate_cols = []
            for t in range(2):
                for s in range(2):
                    gates = g_all[unit, t, s, pl.ds(row, 1), :]
                    gate_cols.append(jnp.broadcast_to(gates, (128, part)).T)
            gate_b = jnp.concatenate(gate_cols, axis=0)
            gate_b = jnp.concatenate([gate_b, gate_b], axis=1)
            start_sum = e == 0
            for c in range(0, d_model, 256):
                o = jnp.dot(inner, down_w[:, c:c + 256], preferred_element_type=jnp.float32)
                o = o.astype(jnp.bfloat16).astype(jnp.float32)
                new = jnp.where(gate_b >= 0.0, gate_b * o, 0.0).reshape(2, 2, part, 256)
                prev = jnp.where(start_sum, 0.0, acc[unit, :, :, :, c:c + 256])
                acc[unit, :, :, :, c:c + 256] = prev + new
            return carry

        lax.fori_loop(0, steps, step_fn, 0)
        reduce_pair(1).start()
        add_pair(1)

        for axis in range(2):
            near = 2 * NEAR + axis
            for t in range(2):
                with jax.named_scope("fin1"):
                    reduce_ring(near, 1 - t).wait_recv()
                rows = pl.ds((2 * axis + t) * part, part)
                acc[axis, t, 0] += stream_ref[rows, :].astype(jnp.float32) + ring_in[2 * (near - 2) + 1 - t]
        for axis in range(2):
            more = 2 * MORE + axis
            for t in range(2):
                with jax.named_scope("fin2"):
                    reduce_ring(more, t).wait_recv()
                rows = pl.ds((2 * axis + t) * part, part)
                out_ref[rows, :] = (acc[axis, t, 0] + ring_in[2 * (more - 2) + t]).astype(out_ref.dtype)
        for unit in range(UNITS):
            wait_send(pair_copy(unit))
            reduce_pair(unit).wait_send()
            if unit >= 2:
                for t in range(2):
                    wait_send(gather(unit % 2, unit // 2, t))
                    reduce_ring(unit, t).wait_send()

    def weight_sends(layer):
        for m in range(3):
            for k in (1, 2, 3):
                pre_copy(layer, m, k).wait_send()
            for p in range(4):
                for r in rounds(layer, m, p):
                    ring_copy(layer, r, m, p).wait_send()

    with jax.named_scope("barrier"):
        pl.semaphore_wait(barrier, len(peers))
    pre_start(0)
    run_layer(0, x_ref)
    for peer in token_peers:
        pl.semaphore_signal(ready, inc=1, device_id=peer, device_id_type=MESH_ID)
    weight_sends(0)
    run_layer(1, out_ref)
    weight_sends(1)


def moe_layers(ring_shape, stream, norm_w, router, routes, weights):
    tok_dev, d_model = stream.shape
    part = tok_dev // 4
    n_z, n_y, n_x = ring_shape
    vmem = pl.BlockSpec(memory_space=pltpu.VMEM)
    hbm = pl.BlockSpec(memory_space=pl.ANY)
    dma = pltpu.SemaphoreType.DMA
    n_exp, f_dev = weights[0].shape[1] // n_x, weights[0].shape[2]
    w_shape = (n_exp, 3, n_z, n_y, n_x, f_dev, d_model)
    return pl.pallas_call(
        functools.partial(kernel, ring_shape),
        name="moe_layers",
        out_shape=[jax.ShapeDtypeStruct(stream.shape, stream.dtype), jax.ShapeDtypeStruct(w_shape, jnp.bfloat16)],
        in_specs=[vmem] * 4 + [hbm] * 3,
        out_specs=[vmem, hbm],
        scratch_shapes=[
            pltpu.VMEM((UNITS, 2, 2, part, d_model), jnp.bfloat16),
            pltpu.VMEM((UNITS, 2, 2, router.shape[1], part), jnp.float32),
            pltpu.VMEM(w_shape, jnp.bfloat16),
            pltpu.VMEM((UNITS, 2, 2, part, d_model), jnp.float32),
            pltpu.VMEM((UNITS, 2, part, d_model), jnp.float32),
            pltpu.VMEM((12, part, d_model), jnp.float32),
            dma((2, 24)), dma((2, 24)), dma((2, 16)), dma((2, 16)), dma((2, 8)), dma((2, 8)), dma((2, 12)), dma((2, 12)),
            dma((6,)), dma((18,)), dma((18,)), dma((144,)), dma((144,)), dma((n_exp,)),
            pltpu.SemaphoreType.REGULAR,
        ],
        compiler_params=pltpu.CompilerParams(
            collective_id=0, has_side_effects=True, vmem_limit_bytes=67043328),
        cost_estimate=pl.CostEstimate(flops=104 * 10**9, bytes_accessed=64 * 2**20, transcendentals=0),
    )(stream, norm_w, router, routes, *weights)[0]


def solution(mesh):
    n_x = 4
    n_y = min(4, mesh.shape["fsdp"] // n_x)
    devices = mesh.devices.reshape(mesh.shape["rep"], mesh.shape["ep"], -1, n_y, n_x)
    cells = Mesh(devices, ("rep", "ep", "z", "y", "x"))
    ring_shape = devices.shape[2:]
    fsdp = ("z", "y", "x")
    token_spec = P(("rep", "ep") + fsdp, None)
    expert_in_spec = P(None, "ep", None, fsdp)
    expert_out_spec = P(None, "ep", fsdp, None)
    route_spec = P(None, ("rep", "ep") + fsdp, None)

    def device_step(x_in, norm_w, router_w, gate_w, up_w, down_w, routes):
        shards = (gate_w.transpose(0, 1, 3, 2), up_w.transpose(0, 1, 3, 2), down_w)
        return moe_layers(ring_shape, x_in, norm_w, router_w.transpose(0, 2, 1), routes.transpose(0, 2, 1), shards)

    return jax.shard_map(device_step, mesh=cells,
                         in_specs=(token_spec, P(), P(), expert_in_spec, expert_in_spec, expert_out_spec, route_spec),
                         out_specs=token_spec, check_vma=False)
```

time: 782 us -> 279 us (0.36); the launches traced: 771 us -> 279 us
  local copies, waits for them, and re-layouts: 406 us -> 2.26 us
  Pallas kernels: 0 us -> 277 us
  waiting for transfers between devices: 135 us -> 0 us
  matrix products: 104 us -> 0 us
  blocking collectives: 53.7 us -> 0 us
  other arithmetic: 45.7 us -> 0 us
  between operations: 14.3 us -> 0.01 us
  starting transfers between devices: 11.4 us -> 0 us
    pallas_call x0 -> x1, Pallas kernels: none -> 277 us  [moe_layers(): pl.pallas_call(functools.partial(kernel, ring_shape), name='moe_layers',...]
    gather x10 -> x0, local copies, waits for them, and re-layouts: 196 us -> none  [the longest x2 70.7 us: device_step(): send_buf = hidden[slot_token].reshape(n_local, owners, capacity, d_model)]
    all_gather x6 -> x0, waiting for transfers between devices: 135 us -> none  [the longest x2 120 us: device_step(): down_full = lax.all_gather(down_w[layer_idx], 'fsdp', axis=1, tiled=True)]
    dot_general x6 -> x0, matrix products: 104 us -> none  [the longest x2 62.6 us: expert_ffn(): jnp.einsum('erf,efd->erd', inner_act, down_full, preferred_element_type=j...]
    all_gather x4 -> x0, local copies, waits for them, and re-layouts: 93.6 us -> none  [the longest x2 46.8 us: device_step(): gate_full = lax.all_gather(gate_w[layer_idx], 'fsdp', axis=2, tiled=True)]
    all_to_all x3 -> x0, blocking collectives: 53.7 us -> none  [the longest x2 36.2 us: device_step(): lax.all_to_all(expert_out.reshape(n_local, owners, capacity, d_model), 'e...]
    reshape x4 -> x0, local copies, waits for them, and re-layouts: 38.4 us -> none  [the longest x2 22 us: device_step(): send_buf = hidden[slot_token].reshape(n_local, owners, capacity, d_model)]
    all_to_all x4 -> x0, local copies, waits for them, and re-layouts: 33.8 us -> none  [the longest x2 20.5 us: device_step(): recv_buf = lax.all_to_all(send_buf, 'ep', 1, 1, tiled=True)]
  transfers between devices with their start and end apart: 7 -> 0, of which waited for: 3 -> 0; matrix products, arithmetic and copies ran while one was open for 61% -> 0% of each run, Pallas kernels for 0% -> 0%
where the time goes in v4:
time: 279 us
  Pallas kernels  277 us (99%)
    pallas_call x1, Pallas kernels, moe_layers(): pl.pallas_call(functools.partial(kernel, ring_shape), name='moe_layers',...  277 us

profile of v4, /device:TPU:1, one launch (start us, length us, event | category | flops | bytes accessed | tf_op | source)
XLA Modules:
  0.0 279.1 jit_solution(7572201647096059885)
XLA Ops:
  0.0 276.8 %moe_layers.1 = (bf16[512,1024]{1,0:T(8,128)(2,1)}, bf16[4,3,4,4,4,8,1024]{6,5,4,3,2,1,0:T(8,128)(2,1)}) custom-call(bf16[512,1024]{1,0:T(8,128)(2,1)} %x_ref.1, f32[2,1024]{1,0:T(2,128)} %norm_ref.1, bf16[2,32,1024]{2,1,0:T(8,128)(2,1)} %bitcast.6, s32[2,8,512]{2,1,0:T(8,128)} %bitcast.7, bf16[2,16,8,1024]{3,2,1,0:T(8,128)(2,1)} %bitcast.4, ...), custom_call_target="tpu_custom_call" | custom-call | flops 103999995904 | bytes 67108864 | tf_op jit(solution)/shard_map/moe_layers/pallas_call | solution.py:400
  276.8 2.3 copy.9

commit v5 on v4

v5 whole, which is shorter than its diff:
```python
import functools

import jax
import jax.numpy as jnp
from jax import lax
from jax.experimental import pallas as pl
from jax.experimental.pallas import tpu as pltpu
from jax.sharding import Mesh, PartitionSpec as P

NORM_EPS = 1e-5
MESH_ID = pl.DeviceIdType.MESH

OWN, NEAR, FAR, MORE = range(4)
UNITS = 8
LATE_EVENTS = (
    ("own", 1, (2, 4)), ("rows", 1, (6, 9)), ("own", 2, (6, 8)),
    ("rest", 0, (11, 16)), ("rest", 1, (19, 27)), ("rest", 2, (32, 35)),
)


def kernel(ring_shape, x_ref, norm_ref, router_ref, routes_ref, gate_ref, up_ref, down_ref, out_ref, next_ref,
           h_all, g_all, w_v, acc, pair_in, ring_in,
           ag_send, ag_recv, agp_send, agp_recv, pair_send, pair_recv, ring_send, ring_recv,
           pre_own, pre_send, pre_recv, wr_send, wr_recv, w_sem, ready):
    part, d_model = h_all.shape[3], h_all.shape[4]
    n_exp = w_v.shape[0]
    n_z, n_y, n_x = ring_shape
    ep, x = lax.axis_index("ep"), lax.axis_index("x")
    z, y = lax.axis_index("z"), lax.axis_index("y")
    partner = {"ep": 1 - ep}
    owners = (x, lax.rem(x + y, 4))
    steps = UNITS * n_exp

    def remote(src, dst, send, recv, peer):
        return pltpu.make_async_remote_copy(src, dst, send, recv, device_id=peer, device_id_type=MESH_ID)

    def beside(layer, axis, stream):
        move = 1 + 2 * stream
        if layer == 0:
            return {"x": lax.rem(x + move, 4)}
        return {"x": lax.rem(x + axis * move, 4), "y": lax.rem(y + (1 - axis) * move, 4)}

    def next_row(layer, step):
        if layer == 0:
            return {"y": lax.rem(y + 4 + step, 4)}
        return {"x": lax.rem(x + 4 - step, 4), "y": lax.rem(y + 4 + step, 4)}

    token_peers = [beside(0, 0, 0), beside(0, 0, 1), beside(1, 0, 0), beside(1, 0, 1), partner]
    peers = token_peers + [{"x": lax.rem(x + 2, 4)}] + [next_row(1, step) for step in (1, -1)]
    if n_z > 1:
        peers += [{"z": lax.rem(z + 1, n_z)}, {"z": lax.rem(z + n_z - 1, n_z)}]
    barrier = pltpu.get_barrier_semaphore()
    for peer in peers:
        pl.semaphore_signal(barrier, inc=1, device_id=peer, device_id_type=MESH_ID)

    sources = (gate_ref, up_ref, down_ref)
    targets = (w_v, next_ref)

    def landing(layer, m):
        return targets[layer].at[:, m, z, 0 if layer else y, x]

    def pre_local(layer, m):
        return pltpu.make_async_copy(
            sources[m].at[layer, pl.ds(owners[layer] * n_exp, n_exp)], landing(layer, m),
            pre_own.at[layer * 3 + m])

    def pre_copy(layer, m, k):
        idx = (layer * 3 + m) * 3 + k - 1
        return remote(sources[m].at[layer, pl.ds(lax.rem(owners[layer] + k, 4) * n_exp, n_exp)],
                      landing(layer, m),
                      pre_send.at[idx], pre_recv.at[idx], {"x": lax.rem(x + k, 4)})

    def hops(along_z):
        return 3 if (n_z if along_z else n_y) > 1 else 0

    def ring_copy(r, m, p):
        step = 1 if p % 2 == 0 else -1
        along_z = (r < 3) == (p < 2)
        if r % 3 >= hops(along_z):
            return None
        pos = z if along_z else y
        i = lax.rem(pos + 4 - step * (r % 3), 4)
        if r < 3:
            piece = w_v.at[p, m, i, y] if along_z else w_v.at[p, m, z, i]
        else:
            piece = w_v.at[p, m, i] if along_z else w_v.at[p, m, :, i]
        idx = (r * 3 + m) * 4 + p
        peer = {"z": lax.rem(z + 4 + step, 4)} if along_z else next_row(0, step)
        return remote(piece, piece, wr_send.at[idx], wr_recv.at[idx], peer)

    def late_copy(stage, hop, m, p):
        if stage == "rows":
            step = 1 - hop % 2 * 2
            near, far = -step % 4, 2
            if hop < 2:
                src, dst = next_ref.at[p, m, z, 0], next_ref.at[p, m, z, near]
            else:
                xs = pl.ds(n_x // 2 * (hop - 2), n_x // 2)
                src, dst = next_ref.at[p, m, z, near, xs], next_ref.at[p, m, z, far, xs]
            peer = next_row(1, step)
        else:
            if hop >= hops(True):
                return None
            step = 1 - p % 2 * 2
            i = lax.rem(z + 4 - step * hop, 4)
            src = dst = next_ref.at[p, m, i, 0 if stage == "own" else pl.ds(1, n_y - 1)]
            peer = {"z": lax.rem(z + 4 + step, 4)}
        idx = 72 + (({"own": 0, "rows": 3, "rest": 7}[stage] + hop) * 3 + m) * 4 + p
        return remote(src, dst, wr_send.at[idx], wr_recv.at[idx], peer)

    def pre_start(layer):
        for m in range(3):
            for k in (1, 3, 2):
                pre_copy(layer, m, k).start()
            pre_local(layer, m).start()

    def pre_wait(layer, m):
        pre_local(layer, m).wait()
        for k in (1, 3, 2):
            pre_copy(layer, m, k).wait_recv()

    def then(before, after):
        if before is not None:
            before.wait_recv()
        if after is not None:
            after.start()

    def ring_event(r, m):
        with jax.named_scope(f"w0r{r}m{m}"):
            if r == 0:
                pre_wait(0, m)
            for p in range(4):
                last = [q for q in range(r) if ring_copy(q, m, p) is not None][-1:]
                after = ring_copy(r, m, p) if r < 6 else None
                if after is not None or r == 6:
                    then(ring_copy(last[0], m, p) if last else None, after)

    def ring_round(r):
        for m in range(3):
            ring_event(r, m)

    def late_event(stage, hop, pair):
        with jax.named_scope(f"w1{stage}{hop}p{pair}"):
            for p in (2 * pair, 2 * pair + 1):
                for m in range(3):
                    before = []
                    after = [late_copy(stage, hop, m, p)]
                    if stage == "rows":
                        before = [late_copy(stage, q, m, p) for q in range(2 * hop)]
                        after = [late_copy(stage, 2 * hop + q, m, p) for q in range(2)]
                    elif hop > 0:
                        before = [late_copy(stage, hop - 1, m, p)]
                    elif stage == "rest":
                        before = [late_copy("rows", q, m, p) for q in (2, 3)]
                    for copy in before:
                        then(copy, None)
                    for copy in after:
                        then(None, copy)

    def late_end(pair):
        with jax.named_scope(f"w1end{pair}"):
            for p in (2 * pair, 2 * pair + 1):
                for m in range(3):
                    then(late_copy("own", 2, m, p), None)
                    then(late_copy("rest", 2, m, p), None)

    loads = [pltpu.make_async_copy(next_ref.at[e], w_v.at[e], w_sem.at[e]) for e in range(n_exp)]

    def prepare(layer, stream_ref, axis):
        experts = router_ref.shape[1]
        for t in range(2):
            rows = pl.ds((2 * axis + t) * part, part)
            wide = stream_ref[rows, :].astype(jnp.float32)
            inv_rms = lax.rsqrt(jnp.mean(wide * wide, axis=-1, keepdims=True) + NORM_EPS)
            hidden = (wide * inv_rms * norm_ref[layer:layer + 1, :]).astype(jnp.bfloat16)
            h_all[axis, t, 0] = hidden
            logits = lax.dot_general(router_ref[layer], hidden, (((1,), (1,)), ((), ())),
                                     preferred_element_type=jnp.float32)
            ids = lax.broadcasted_iota(jnp.int32, (experts, part), 0)
            chosen = ids < 0
            for j in range(routes_ref.shape[1]):
                chosen |= routes_ref[layer, j:j + 1, (2 * axis + t) * part:(2 * axis + t + 1) * part] == ids
            top = jnp.max(jnp.where(chosen, logits, -jnp.inf), axis=0, keepdims=True)
            weight = jnp.where(chosen, jnp.exp(jnp.where(chosen, logits - top, 0.0)), 0.0)
            gates = weight / jnp.sum(weight, axis=0, keepdims=True)
            g_all[axis, t, 0] = jnp.where(chosen, gates, -1.0)

    def start(copies):
        for copy in copies:
            copy.start()

    def wait_recv(copies):
        for copy in copies:
            copy.wait_recv()

    def wait_send(copies):
        for copy in copies:
            copy.wait_send()

    def run_layer(layer, stream_ref, halfway=None):
        first = layer == 0
        group = ep * 4 + owners[layer]

        def pair_copy(unit):
            return (
                remote(h_all.at[unit, :, 0], h_all.at[unit, :, 1],
                       agp_send.at[layer, unit], agp_recv.at[layer, unit], partner),
                remote(g_all.at[unit, :, 0], g_all.at[unit, :, 1],
                       agp_send.at[layer, 8 + unit], agp_recv.at[layer, 8 + unit], partner),
            )

        def gather(axis, kind, t):
            src_kind, src_t, to = {
                (NEAR, 1): (OWN, 0, 0), (MORE, 1): (OWN, 1, 0), (FAR, 0): (NEAR, 1, 0),
                (NEAR, 0): (OWN, 1, 1), (MORE, 0): (OWN, 0, 1), (FAR, 1): (NEAR, 0, 1),
            }[kind, t]
            src, dst = 2 * src_kind + axis, 2 * kind + axis
            idx = 2 * (dst - 2) + t
            peer = beside(layer, axis, to)
            return (
                remote(h_all.at[src, src_t, 0], h_all.at[dst, t, 0],
                       ag_send.at[layer, idx], ag_recv.at[layer, idx], peer),
                remote(g_all.at[src, src_t, 0], g_all.at[dst, t, 0],
                       ag_send.at[layer, 12 + idx], ag_recv.at[layer, 12 + idx], peer),
            )

        def gather_start(axis):
            for t in range(2):
                start(gather(axis, NEAR, t))
            start(pair_copy(axis))
            for t in range(2):
                start(gather(axis, MORE, t))

        def arrive(kind, axis):
            with jax.named_scope(f"arr{kind}{axis}"):
                for t in range(2):
                    wait_recv(gather(axis, kind, t))
                    if kind == NEAR:
                        start(gather(axis, FAR, 1 - t))
                start(pair_copy(2 * kind + axis))

        def reduce_pair(unit):
            return remote(acc.at[unit, :, 1], pair_in.at[unit],
                          pair_send.at[layer, unit], pair_recv.at[layer, unit], partner)

        def place(unit, t):
            return 2 * (unit - 2) + t + 4 * layer * (unit // 6)

        def reduce_ring(unit, t):
            slot = 2 * (unit - 2) + t
            return remote(acc.at[unit, t, 0], ring_in.at[place(unit, t)], ring_send.at[layer, slot], ring_recv.at[layer, slot],
                          beside(layer, unit % 2, t))

        def add_pair(unit):
            with jax.named_scope("pairw"):
                reduce_pair(unit).wait_recv()
            acc[unit, :, 0] += pair_in[unit]

        def add_more(unit):
            with jax.named_scope("morew"):
                reduce_pair(unit).wait_recv()
                far = unit - 2 * (MORE - FAR)
                for t in range(2):
                    reduce_ring(far, t).wait_recv()
            for t in range(2):
                acc[unit, t, 0] += pair_in[unit, t] + ring_in[place(far, t)]

        def ring_start(unit):
            for t in range(2):
                reduce_ring(unit, t).start()

        plan = {}

        def at(t, action, *args):
            plan.setdefault(t, []).append((action, args))

        if first:
            for axis in range(2):
                prepare(layer, stream_ref, axis)
            for kind in (NEAR, MORE):
                for axis in range(2):
                    for t in range(2):
                        start(gather(axis, kind, t))
                    if kind == NEAR:
                        start(pair_copy(axis))
        else:
            prepare(layer, stream_ref, 0)
            with jax.named_scope("ready"):
                pl.semaphore_wait(ready, len(token_peers))
            gather_start(0)
        if first:
            for r in range(3):
                ring_round(r)
            arrive(NEAR, 0)
            arrive(NEAR, 1)
            pre_start(1)
            ring_round(3)
            ring_round(4)
            arrive(MORE, 0)
            arrive(MORE, 1)
            ring_round(5)
            arrive(FAR, 0)
            arrive(FAR, 1)
            ring_event(6, 0)
            ring_event(6, 1)
            for m in range(3):
                pre_wait(1, m)
            for pair in range(2):
                late_event("own", 0, pair)
            ring_event(6, 2)
            for pair in range(2):
                late_event("rows", 0, pair)
            for unit in range(UNITS):
                wait_recv(pair_copy(unit))
            for stage, hop, when in LATE_EVENTS:
                for pair in range(2):
                    at(when[pair], late_event, stage, hop, pair)
        else:
            halfway()
            prepare(layer, stream_ref, 1)
            gather_start(1)
            late_end(0)
            start(loads[:2])
            at(0, loads[0].wait)
            at(1, loads[1].wait)
            at(1, late_end, 1)
            at(1, start, loads[2:])
            at(2, loads[2].wait)
            at(3, loads[3].wait)

            for axis in range(2):
                at(3, arrive, NEAR, axis)
                at(6, arrive, MORE, axis)
                at(9, arrive, FAR, axis)

        def unit_of(k):
            if first:
                return jnp.where(k < 2, k + 2 * FAR, jnp.where(k < 4, k, jnp.where(k < 6, k + 2, k - 6)))
            return jnp.where(k == 0, 0, jnp.where(k == UNITS - 1, 1, k + 1))

        def step_fn(step, carry):
            k, e = step // n_exp, step % n_exp
            before, late = unit_of(k - 1), unit_of(k - 2)
            kind, late_kind = before // 2, late // 2

            def planned(e_static):
                for t in sorted(plan):
                    if t < steps and t % n_exp == e_static:
                        @pl.when(k == t // n_exp)
                        def _():
                            for action, args in plan[t]:
                                action(*args)

            @pl.when(e == 0)
            def _():
                planned(0)

                @pl.when(k >= 1)
                def _():
                    reduce_pair(before).start()

                if not first:
                    wait_recv(pair_copy(unit_of(k)))

            def sums(mask):
                @pl.when(mask & (k >= 1) & (kind != MORE))
                def _():
                    add_pair(before)

                @pl.when(mask & ((k >= 2) & (late_kind == MORE) if first else (k >= 1) & (kind == MORE)))
                def _():
                    add_more(late if first else before)

            def leave(mask):
                @pl.when(mask & (k >= 1) & (kind != OWN) & ((kind != MORE) if first else True))
                def _():
                    ring_start(before)

                if first:
                    @pl.when(mask & (k >= 2) & (late_kind == MORE))
                    def _():
                        ring_start(late)

            hurry = k == 1 if first else (k == 4) | (k == 5) | (k == UNITS - 1)

            @pl.when(e == 1)
            def _():
                planned(1)
                sums(hurry)

            @pl.when(e == 2)
            def _():
                planned(2)
                sums(jnp.logical_not(hurry))
                leave(hurry)

            @pl.when(e == 3)
            def _():
                planned(3)
                leave(jnp.logical_not(hurry))

            unit = unit_of(k)
            with jax.named_scope("load"):
                tokens = h_all[unit].reshape(-1, d_model)
            gate_w = w_v[e, 0].reshape(-1, d_model)
            up_w = w_v[e, 1].reshape(-1, d_model)
            down_w = w_v[e, 2].reshape(-1, d_model)
            d_ff = gate_w.shape[0]
            inner = []
            for f in range(0, d_ff, 256):
                nt = (((1,), (1,)), ((), ()))
                u = lax.dot_general(tokens, gate_w[f:f + 256], nt, preferred_element_type=jnp.float32)
                v = lax.dot_general(tokens, up_w[f:f + 256], nt, preferred_element_type=jnp.float32)
                inner.append((jax.nn.silu(u) * v).astype(jnp.bfloat16))
            inner = jnp.concatenate(inner, axis=1)
            row = group * n_exp + e
            gate_cols = []
            for t in range(2):
                for s in range(2):
                    gates = g_all[unit, t, s, pl.ds(row, 1), :]
                    gate_cols.append(jnp.broadcast_to(gates, (128, part)).T)
            gate_b = jnp.concatenate(gate_cols, axis=0)
            gate_b = jnp.concatenate([gate_b, gate_b], axis=1)
            start_sum = e == 0
            for c in range(0, d_model, 256):
                o = jnp.dot(inner, down_w[:, c:c + 256], preferred_element_type=jnp.float32)
                o = o.astype(jnp.bfloat16).astype(jnp.float32)
                new = jnp.where(gate_b >= 0.0, gate_b * o, 0.0).reshape(2, 2, part, 256)
                prev = jnp.where(start_sum, 0.0, acc[unit, :, :, :, c:c + 256])
                acc[unit, :, :, :, c:c + 256] = prev + new
            return carry

        lax.fori_loop(0, steps, step_fn, 0)
        reduce_pair(1).start()
        for t in sorted(plan):
            if t >= steps:
                for action, args in plan[t]:
                    action(*args)
        add_pair(1)

        def end_near(axis):
            near = 2 * NEAR + axis
            for t in range(2):
                with jax.named_scope("fin1"):
                    reduce_ring(near, 1 - t).wait_recv()
                rows = pl.ds((2 * axis + t) * part, part)
                acc[axis, t, 0] += stream_ref[rows, :].astype(jnp.float32) + ring_in[place(near, 1 - t)]

        def end_more(axis):
            more = 2 * MORE + axis
            for t in range(2):
                with jax.named_scope("fin2"):
                    reduce_ring(more, t).wait_recv()
                rows = pl.ds((2 * axis + t) * part, part)
                out_ref[rows, :] = (acc[axis, t, 0] + ring_in[place(more, t)]).astype(out_ref.dtype)

        def end_sends():
            for axis in range(2):
                for t in range(2):
                    reduce_ring(2 * MORE + axis, t).wait_send()

        end_near(0)
        end_near(1)
        for unit in range(UNITS):
            wait_send(pair_copy(unit))
            reduce_pair(unit).wait_send()
            if unit >= 2:
                for t in range(2):
                    wait_send(gather(unit % 2, unit // 2, t))
                    if unit < 2 * MORE:
                        reduce_ring(unit, t).wait_send()
        return end_more, end_sends

    def weight_sends(layer):
        for m in range(3):
            for k in (1, 2, 3):
                pre_copy(layer, m, k).wait_send()
            for p in range(4):
                if layer == 0:
                    copies = [ring_copy(r, m, p) for r in range(6)]
                else:
                    copies = [late_copy(stage, hop, m, p) for stage in ("own", "rest") for hop in range(3)]
                    copies += [late_copy("rows", hop, m, p) for hop in range(4)]
                wait_send([copy for copy in copies if copy is not None])

    with jax.named_scope("barrier"):
        pl.semaphore_wait(barrier, len(peers))
    pre_start(0)
    end_more, end_sends = run_layer(0, x_ref)
    weight_sends(0)
    for peer in token_peers:
        pl.semaphore_signal(ready, inc=1, device_id=peer, device_id_type=MESH_ID)
    end_more(0)

    def halfway():
        end_more(1)
        end_sends()

    end_more_1, end_sends_1 = run_layer(1, out_ref, halfway)
    end_more_1(0)
    end_more_1(1)
    end_sends_1()
    weight_sends(1)


def moe_layers(ring_shape, stream, norm_w, router, routes, weights):
    tok_dev, d_model = stream.shape
    part = tok_dev // 4
    n_z, n_y, n_x = ring_shape
    vmem = pl.BlockSpec(memory_space=pltpu.VMEM)
    hbm = pl.BlockSpec(memory_space=pl.ANY)
    dma = pltpu.SemaphoreType.DMA
    n_exp, f_dev = weights[0].shape[1] // n_x, weights[0].shape[2]
    w_shape = (n_exp, 3, n_z, n_y, n_x, f_dev, d_model)
    return pl.pallas_call(
        functools.partial(kernel, ring_shape),
        name="moe_layers",
        out_shape=[jax.ShapeDtypeStruct(stream.shape, stream.dtype), jax.ShapeDtypeStruct(w_shape, jnp.bfloat16)],
        in_specs=[vmem] * 4 + [hbm] * 3,
        out_specs=[vmem, hbm],
        scratch_shapes=[
            pltpu.VMEM((UNITS, 2, 2, part, d_model), jnp.bfloat16),
            pltpu.VMEM((UNITS, 2, 2, router.shape[1], part), jnp.float32),
            pltpu.VMEM(w_shape, jnp.bfloat16),
            pltpu.VMEM((UNITS, 2, 2, part, d_model), jnp.float32),
            pltpu.VMEM((UNITS, 2, part, d_model), jnp.float32),
            pltpu.VMEM((16, part, d_model), jnp.float32),
            dma((2, 24)), dma((2, 24)), dma((2, 16)), dma((2, 16)), dma((2, 8)), dma((2, 8)), dma((2, 12)), dma((2, 12)),
            dma((6,)), dma((18,)), dma((18,)), dma((192,)), dma((192,)), dma((n_exp,)),
            pltpu.SemaphoreType.REGULAR,
        ],
        compiler_params=pltpu.CompilerParams(
            collective_id=0, has_side_effects=True, vmem_limit_bytes=67043328),
        cost_estimate=pl.CostEstimate(flops=104 * 10**9, bytes_accessed=64 * 2**20, transcendentals=0),
    )(stream, norm_w, router, routes, *weights)[0]


def solution(mesh):
    n_x = 4
    n_y = min(4, mesh.shape["fsdp"] // n_x)
    devices = mesh.devices.reshape(mesh.shape["rep"], mesh.shape["ep"], -1, n_y, n_x)
    cells = Mesh(devices, ("rep", "ep", "z", "y", "x"))
    ring_shape = devices.shape[2:]
    fsdp = ("z", "y", "x")
    token_spec = P(("rep", "ep") + fsdp, None)
    expert_in_spec = P(None, "ep", None, fsdp)
    expert_out_spec = P(None, "ep", fsdp, None)
    route_spec = P(None, ("rep", "ep") + fsdp, None)

    def device_step(x_in, norm_w, router_w, gate_w, up_w, down_w, routes):
        shards = (gate_w.transpose(0, 1, 3, 2), up_w.transpose(0, 1, 3, 2), down_w)
        return moe_layers(ring_shape, x_in, norm_w, router_w.transpose(0, 2, 1), routes.transpose(0, 2, 1), shards)

    return jax.shard_map(device_step, mesh=cells,
                         in_specs=(token_spec, P(), P(), expert_in_spec, expert_in_spec, expert_out_spec, route_spec),
                         out_specs=token_spec, check_vma=False)
```

time: 279 us -> 270 us (0.968)
  Pallas kernels: 277 us -> 267 us
    pallas_call x1, Pallas kernels: 277 us -> 267 us  [moe_layers(): pl.pallas_call(functools.partial(kernel, ring_shape), name='moe_layers',...]
where the time goes in v5:
time: 270 us
  Pallas kernels  267 us (99%)
    pallas_call x1, Pallas kernels, moe_layers(): pl.pallas_call(functools.partial(kernel, ring_shape), name='moe_layers',...  267 us

profile of v5, /device:TPU:1, one launch (start us, length us, event | category | flops | bytes accessed | tf_op | source)
XLA Modules:
  0.0 269.7 jit_solution(10997860383627686522)
XLA Ops:
  0.0 267.4 %moe_layers.1 = (bf16[512,1024]{1,0:T(8,128)(2,1)}, bf16[4,3,4,4,4,8,1024]{6,5,4,3,2,1,0:T(8,128)(2,1)}) custom-call(bf16[512,1024]{1,0:T(8,128)(2,1)} %x_ref.1, f32[2,1024]{1,0:T(2,128)} %norm_ref.1, bf16[2,32,1024]{2,1,0:T(8,128)(2,1)} %bitcast.6, s32[2,8,512]{2,1,0:T(8,128)} %bitcast.7, bf16[2,16,8,1024]{3,2,1,0:T(8,128)(2,1)} %bitcast.4, ...), custom_call_target="tpu_custom_call" | custom-call | flops 103999995904 | bytes 67108864 | tf_op jit(solution)/shard_map/moe_layers/pallas_call | solution.py:515
  267.4 2.3 copy.9

commit v6 on v5

--- a/solution.py
+++ b/solution.py
@@ -88,24 +88,24 @@
         peer = {"z": lax.rem(z + 4 + step, 4)} if along_z else next_row(0, step)
         return remote(piece, piece, wr_send.at[idx], wr_recv.at[idx], peer)
 
-    def late_copy(stage, hop, m, p):
+    def late_copy(stage, hop, p):
         if stage == "rows":
             step = 1 - hop % 2 * 2
             near, far = -step % 4, 2
             if hop < 2:
-                src, dst = next_ref.at[p, m, z, 0], next_ref.at[p, m, z, near]
+                src, dst = next_ref.at[p, :, z, 0], next_ref.at[p, :, z, near]
             else:
                 xs = pl.ds(n_x // 2 * (hop - 2), n_x // 2)
-                src, dst = next_ref.at[p, m, z, near, xs], next_ref.at[p, m, z, far, xs]
+                src, dst = next_ref.at[p, :, z, near, xs], next_ref.at[p, :, z, far, xs]
             peer = next_row(1, step)
         else:
             if hop >= hops(True):
                 return None
             step = 1 - p % 2 * 2
             i = lax.rem(z + 4 - step * hop, 4)
-            src = dst = next_ref.at[p, m, i, 0 if stage == "own" else pl.ds(1, n_y - 1)]
+            src = dst = next_ref.at[p, :, i, 0 if stage == "own" else pl.ds(1, n_y - 1)]
             peer = {"z": lax.rem(z + 4 + step, 4)}
-        idx = 72 + (({"own": 0, "rows": 3, "rest": 7}[stage] + hop) * 3 + m) * 4 + p
+        idx = 72 + ({"own": 0, "rows": 3, "rest": 7}[stage] + hop) * 4 + p
         return remote(src, dst, wr_send.at[idx], wr_recv.at[idx], peer)
 
     def pre_start(layer):
@@ -142,27 +142,25 @@
     def late_event(stage, hop, pair):
         with jax.named_scope(f"w1{stage}{hop}p{pair}"):
             for p in (2 * pair, 2 * pair + 1):
-                for m in range(3):
-                    before = []
-                    after = [late_copy(stage, hop, m, p)]
-                    if stage == "rows":
-                        before = [late_copy(stage, q, m, p) for q in range(2 * hop)]
-                        after = [late_copy(stage, 2 * hop + q, m, p) for q in range(2)]
-                    elif hop > 0:
-                        before = [late_copy(stage, hop - 1, m, p)]
-                    elif stage == "rest":
-                        before = [late_copy("rows", q, m, p) for q in (2, 3)]
-                    for copy in before:
-                        then(copy, None)
-                    for copy in after:
-                        then(None, copy)
+                before = []
+                after = [late_copy(stage, hop, p)]
+                if stage == "rows":
+                    before = [late_copy(stage, q, p) for q in range(2 * hop)]
+                    after = [late_copy(stage, 2 * hop + q, p) for q in range(2)]
+                elif hop > 0:
+                    before = [late_copy(stage, hop - 1, p)]
+                elif stage == "rest":
+                    before = [late_copy("rows", q, p) for q in (2, 3)]
+                for copy in before:
+                    then(copy, None)
+                for copy in after:
+                    then(None, copy)
 
     def late_end(pair):
         with jax.named_scope(f"w1end{pair}"):
             for p in (2 * pair, 2 * pair + 1):
-                for m in range(3):
-                    then(late_copy("own", 2, m, p), None)
-                    then(late_copy("rest", 2, m, p), None)
+                then(late_copy("own", 2, p), None)
+                then(late_copy("rest", 2, p), None)
 
     loads = [pltpu.make_async_copy(next_ref.at[e], w_v.at[e], w_sem.at[e]) for e in range(n_exp)]
 
@@ -197,6 +195,34 @@
         for copy in copies:
             copy.wait_send()
 
+    def early_sends():
+        for m in range(3):
+            for k in (1, 2, 3):
+                pre_copy(0, m, k).wait_send()
+            for p in range(4):
+                wait_send([copy for copy in (ring_copy(r, m, p) for r in range(6)) if copy is not None])
+
+    def late_sends(last):
+        for p in range(4):
+            copies = [late_copy("rest", 2, p)]
+            if not last:
+                copies = [late_copy(stage, hop, p) for stage in ("own", "rest") for hop in range(3)][:5]
+                copies += [late_copy("rows", hop, p) for hop in range(4)]
+            wait_send([copy for copy in copies if copy is not None])
+        if not last:
+            for m in range(3):
+                for k in (1, 2, 3):
+                    pre_copy(1, m, k).wait_send()
+
+    def by_rows(update):
+        chunk = min(32, part)
+
+        def body(i, carry):
+            update(pl.ds(pl.multiple_of(i * chunk, chunk), chunk), i * chunk, chunk)
+            return carry
+
+        lax.fori_loop(0, part // chunk, body, 0)
+
     def run_layer(layer, stream_ref, halfway=None):
         first = layer == 0
         group = ep * 4 + owners[layer]
@@ -204,9 +230,9 @@
         def pair_copy(unit):
             return (
                 remote(h_all.at[unit, :, 0], h_all.at[unit, :, 1],
-                       agp_send.at[layer, unit], agp_recv.at[layer, unit], partner),
+                       agp_send.at[unit], agp_recv.at[unit], partner),
                 remote(g_all.at[unit, :, 0], g_all.at[unit, :, 1],
-                       agp_send.at[layer, 8 + unit], agp_recv.at[layer, 8 + unit], partner),
+                       agp_send.at[8 + unit], agp_recv.at[8 + unit], partner),
             )
 
         def gather(axis, kind, t):
@@ -219,9 +245,9 @@
             peer = beside(layer, axis, to)
             return (
                 remote(h_all.at[src, src_t, 0], h_all.at[dst, t, 0],
-                       ag_send.at[layer, idx], ag_recv.at[layer, idx], peer),
+                       ag_send.at[idx], ag_recv.at[idx], peer),
                 remote(g_all.at[src, src_t, 0], g_all.at[dst, t, 0],
-                       ag_send.at[layer, 12 + idx], ag_recv.at[layer, 12 + idx], peer),
+                       ag_send.at[12 + idx], ag_recv.at[12 + idx], peer),
             )
 
         def gather_start(axis):
@@ -241,7 +267,7 @@
 
         def reduce_pair(unit):
             return remote(acc.at[unit, :, 1], pair_in.at[unit],
-                          pair_send.at[layer, unit], pair_recv.at[layer, unit], partner)
+                          pair_send.at[unit], pair_recv.at[unit], partner)
 
         def place(unit, t):
             return 2 * (unit - 2) + t + 4 * layer * (unit // 6)
@@ -254,7 +280,12 @@
         def add_pair(unit):
             with jax.named_scope("pairw"):
                 reduce_pair(unit).wait_recv()
-            acc[unit, :, 0] += pair_in[unit]
+
+            def update(rows, first_row, n):
+                for t in range(2):
+                    acc[unit, t, 0, rows] += pair_in[unit, t, rows]
+
+            by_rows(update)
 
         def add_more(unit):
             with jax.named_scope("morew"):
@@ -262,8 +293,12 @@
                 far = unit - 2 * (MORE - FAR)
                 for t in range(2):
                     reduce_ring(far, t).wait_recv()
-            for t in range(2):
-                acc[unit, t, 0] += pair_in[unit, t] + ring_in[place(far, t)]
+
+            def update(rows, first_row, n):
+                for t in range(2):
+                    acc[unit, t, 0, rows] += pair_in[unit, t, rows] + ring_in[place(far, t), rows]
+
+            by_rows(update)
 
         def ring_start(unit):
             for t in range(2):
@@ -321,22 +356,21 @@
             gather_start(1)
             late_end(0)
             start(loads[:2])
-            at(0, loads[0].wait)
-            at(1, loads[1].wait)
-            at(1, late_end, 1)
-            at(1, start, loads[2:])
-            at(2, loads[2].wait)
-            at(3, loads[3].wait)
-
+            late_sends(last=False)
             for axis in range(2):
-                at(3, arrive, NEAR, axis)
-                at(6, arrive, MORE, axis)
-                at(9, arrive, FAR, axis)
+                arrive(NEAR, axis)
+            late_end(1)
+            start(loads[2:])
+            for e in range(n_exp):
+                at(e, loads[e].wait)
+            for axis in range(2):
+                at(3, arrive, MORE, axis)
+                at(5, arrive, FAR, axis)
 
         def unit_of(k):
             if first:
                 return jnp.where(k < 2, k + 2 * FAR, jnp.where(k < 4, k, jnp.where(k < 6, k + 2, k - 6)))
-            return jnp.where(k == 0, 0, jnp.where(k == UNITS - 1, 1, k + 1))
+            return jnp.where(k < 6, k + 2, k - 6)
 
         def step_fn(step, carry):
             k, e = step // n_exp, step % n_exp
@@ -381,7 +415,7 @@
                     def _():
                         ring_start(late)
 
-            hurry = k == 1 if first else (k == 4) | (k == 5) | (k == UNITS - 1)
+            hurry = k == 1 if first else (k == 4) | (k == 6)
 
             @pl.when(e == 1)
             def _():
@@ -436,23 +470,30 @@
             if t >= steps:
                 for action, args in plan[t]:
                     action(*args)
-        add_pair(1)
 
         def end_near(axis):
             near = 2 * NEAR + axis
             for t in range(2):
                 with jax.named_scope("fin1"):
                     reduce_ring(near, 1 - t).wait_recv()
-                rows = pl.ds((2 * axis + t) * part, part)
-                acc[axis, t, 0] += stream_ref[rows, :].astype(jnp.float32) + ring_in[place(near, 1 - t)]
+
+                def update(rows, first_row, n):
+                    own = pl.ds(pl.multiple_of((2 * axis + t) * part + first_row, n), n)
+                    acc[axis, t, 0, rows] += stream_ref[own, :].astype(jnp.float32) + ring_in[place(near, 1 - t), rows]
+
+                by_rows(update)
 
         def end_more(axis):
             more = 2 * MORE + axis
             for t in range(2):
                 with jax.named_scope("fin2"):
                     reduce_ring(more, t).wait_recv()
-                rows = pl.ds((2 * axis + t) * part, part)
-                out_ref[rows, :] = (acc[axis, t, 0] + ring_in[place(more, t)]).astype(out_ref.dtype)
+
+                def update(rows, first_row, n):
+                    own = pl.ds(pl.multiple_of((2 * axis + t) * part + first_row, n), n)
+                    out_ref[own, :] = (acc[axis, t, 0, rows] + ring_in[place(more, t), rows]).astype(out_ref.dtype)
+
+                by_rows(update)
 
         def end_sends():
             for axis in range(2):
@@ -460,6 +501,9 @@
                     reduce_ring(2 * MORE + axis, t).wait_send()
 
         end_near(0)
+        if not first:
+            end_more(0)
+        add_pair(1)
         end_near(1)
         for unit in range(UNITS):
             wait_send(pair_copy(unit))
@@ -471,23 +515,11 @@
                         reduce_ring(unit, t).wait_send()
         return end_more, end_sends
 
-    def weight_sends(layer):
-        for m in range(3):
-            for k in (1, 2, 3):
-                pre_copy(layer, m, k).wait_send()
-            for p in range(4):
-                if layer == 0:
-                    copies = [ring_copy(r, m, p) for r in range(6)]
-                else:
-                    copies = [late_copy(stage, hop, m, p) for stage in ("own", "rest") for hop in range(3)]
-                    copies += [late_copy("rows", hop, m, p) for hop in range(4)]
-                wait_send([copy for copy in copies if copy is not None])
-
     with jax.named_scope("barrier"):
         pl.semaphore_wait(barrier, len(peers))
     pre_start(0)
     end_more, end_sends = run_layer(0, x_ref)
-    weight_sends(0)
+    early_sends()
     for peer in token_peers:
         pl.semaphore_signal(ready, inc=1, device_id=peer, device_id_type=MESH_ID)
     end_more(0)
@@ -497,10 +529,9 @@
         end_sends()
 
     end_more_1, end_sends_1 = run_layer(1, out_ref, halfway)
-    end_more_1(0)
     end_more_1(1)
     end_sends_1()
-    weight_sends(1)
+    late_sends(last=True)
 
 
 def moe_layers(ring_shape, stream, norm_w, router, routes, weights):
@@ -525,8 +556,8 @@
             pltpu.VMEM((UNITS, 2, 2, part, d_model), jnp.float32),
             pltpu.VMEM((UNITS, 2, part, d_model), jnp.float32),
             pltpu.VMEM((16, part, d_model), jnp.float32),
-            dma((2, 24)), dma((2, 24)), dma((2, 16)), dma((2, 16)), dma((2, 8)), dma((2, 8)), dma((2, 12)), dma((2, 12)),
-            dma((6,)), dma((18,)), dma((18,)), dma((192,)), dma((192,)), dma((n_exp,)),
+            dma((24,)), dma((24,)), dma((16,)), dma((16,)), dma((8,)), dma((8,)), dma((2, 12)), dma((2, 12)),
+            dma((6,)), dma((18,)), dma((18,)), dma((112,)), dma((112,)), dma((n_exp,)),
             pltpu.SemaphoreType.REGULAR,
         ],
         compiler_params=pltpu.CompilerParams(

time: 270 us -> 263 us (0.974)
  Pallas kernels: 267 us -> 261 us
    pallas_call x1, Pallas kernels: 267 us -> 261 us  [moe_layers(): pl.pallas_call(functools.partial(kernel, ring_shape), name='moe_layers',...]
where the time goes in v6:
time: 263 us
  Pallas kernels  261 us (99%)
    pallas_call x1, Pallas kernels, moe_layers(): pl.pallas_call(functools.partial(kernel, ring_shape), name='moe_layers',...  261 us

profile of v6, /device:TPU:1, one launch (start us, length us, event | category | flops | bytes accessed | tf_op | source)
XLA Modules:
  0.0 263.2 jit_solution(3217325351068195520)
XLA Ops:
  0.0 261.0 %moe_layers.1 = (bf16[512,1024]{1,0:T(8,128)(2,1)}, bf16[4,3,4,4,4,8,1024]{6,5,4,3,2,1,0:T(8,128)(2,1)}) custom-call(bf16[512,1024]{1,0:T(8,128)(2,1)} %x_ref.1, f32[2,1024]{1,0:T(2,128)} %norm_ref.1, bf16[2,32,1024]{2,1,0:T(8,128)(2,1)} %bitcast.6, s32[2,8,512]{2,1,0:T(8,128)} %bitcast.7, bf16[2,16,8,1024]{3,2,1,0:T(8,128)(2,1)} %bitcast.4, ...), custom_call_target="tpu_custom_call" | custom-call | flops 103999995904 | bytes 67108864 | tf_op jit(solution)/shard_map/moe_layers/pallas_call | solution.py:546
  261.0 2.3 copy.9

commit v7 on v6

--- a/solution.py
+++ b/solution.py
@@ -357,15 +357,18 @@
             late_end(0)
             start(loads[:2])
             late_sends(last=False)
-            for axis in range(2):
-                arrive(NEAR, axis)
-            late_end(1)
-            start(loads[2:])
-            for e in range(n_exp):
-                at(e, loads[e].wait)
-            for axis in range(2):
-                at(3, arrive, MORE, axis)
-                at(5, arrive, FAR, axis)
+            arrive(NEAR, 0)
+            at(0, loads[0].wait)
+            at(1, loads[1].wait)
+            at(1, late_end, 1)
+            at(1, start, loads[2:])
+            at(1, arrive, NEAR, 1)
+            at(2, loads[2].wait)
+            at(3, loads[3].wait)
+            at(3, arrive, MORE, 0)
+            at(3, arrive, MORE, 1)
+            at(5, arrive, FAR, 0)
+            at(7, arrive, FAR, 1)
 
         def unit_of(k):
             if first:

time: 263 us -> 262 us (level)
  no operation moved by 1% of the time
where the time goes in v7:
time: 262 us
  Pallas kernels  260 us (99%)
    pallas_call x1, Pallas kernels, moe_layers(): pl.pallas_call(functools.partial(kernel, ring_shape), name='moe_layers',...  260 us

profile of v7, /device:TPU:1, one launch (start us, length us, event | category | flops | bytes accessed | tf_op | source)
XLA Modules:
  0.0 261.9 jit_solution(727941026008719755)
XLA Ops:
  0.0 259.7 %moe_layers.1 = (bf16[512,1024]{1,0:T(8,128)(2,1)}, bf16[4,3,4,4,4,8,1024]{6,5,4,3,2,1,0:T(8,128)(2,1)}) custom-call(bf16[512,1024]{1,0:T(8,128)(2,1)} %x_ref.1, f32[2,1024]{1,0:T(2,128)} %norm_ref.1, bf16[2,32,1024]{2,1,0:T(8,128)(2,1)} %bitcast.6, s32[2,8,512]{2,1,0:T(8,128)} %bitcast.7, bf16[2,16,8,1024]{3,2,1,0:T(8,128)(2,1)} %bitcast.4, ...), custom_call_target="tpu_custom_call" | custom-call | flops 103999995904 | bytes 67108864 | tf_op jit(solution)/shard_map/moe_layers/pallas_call | solution.py:549
  259.7 2.3 copy.9
